TPU v7x, 256 devices: a whole 4x4x8 slice. The times are simulated.
256 devices in a mesh: section: 4 (over y_lo, core), lon: 32 (over z, x), lat: 2 (over y_hi).
Axes of the slice: x: 4, y: 4 (y_hi: 2, y_lo: 2; y = y_hi * 2 + y_lo), z: 8, core: 2. Of those that a mesh axis runs over, the one named last changes fastest.
Arguments:
- inputs: bfloat16 [4, 8, 12, 384, 192], P('section', None, 'lat', 'lon'), may hold values from -6 to 6
- grad_output: bfloat16 [4, 8, 12, 384, 192], P('section', None, 'lat', 'lon'), may hold values from -6 to 6
- norm_gains: float32 [4, 2, 2, 192], P('section'), may hold values from 0.25 to 1.75
- input_weight: bfloat16 [4, 2, 192, 576], P('section'), may hold values from -0.4375 to 0.4375
- output_weight: bfloat16 [4, 2, 192, 192], P('section'), may hold values from -0.4375 to 0.4375
- expand_weight: bfloat16 [4, 2, 192, 768], P('section'), may hold values from -0.4375 to 0.4375
- reduce_weight: bfloat16 [4, 2, 768, 192], P('section'), may hold values from -0.21875 to 0.21875
- bias_table: float32 [4, 2, 4, 2, 6, 3312], P('section'), may hold values from -4 to 400
Outputs:
- upstream: bfloat16 [4, 8, 12, 384, 192], P('section', None, 'lat', 'lon')
- input_weight_grad: float32 [4, 2, 192, 576], P('section')
- output_weight_grad: float32 [4, 2, 192, 192], P('section')
- expand_weight_grad: float32 [4, 2, 192, 768], P('section')
- reduce_weight_grad: float32 [4, 2, 768, 192], P('section')
- norm_gain_grad: float32 [4, 2, 2, 192], P('section')
- bias_table_grad: float32 [4, 2, 4, 2, 6, 3312], P('section')
All inputs are finite; a program needn't handle non-finite values.
Results may differ from a plain program's by a relative error of at most 0.04.
Values may be sent and summed in bfloat16 or wider, within the bound.
No kernel may reach another device: no remote copies, remote signals or barrier semaphores. Data moves between devices by JAX's collectives and lax.ppermute only.
A program may use at most 128 MiB of HBM per device.

v0:
```python
import jax
import jax.numpy as jnp
from jax import lax
from jax.sharding import PartitionSpec as P

MODEL_WIDTH = 192
HEADS = 6
HEAD_SIZE = 32
LEVELS = 8
WIN_LEVELS = 2
WIN_LAT = 6
WIN_LON = 12
BLOCKS = 2
LAT_DEV = 6
LON_DEV = 12
WIN_TOKENS = 144
BIAS_SLOTS = 3312


NORM_EPS = 1e-05
MASK_FILL = -10000.0


def swapped(value, axis, stride):
    mask = 2**stride
    pairs = [(source, source ^ mask) for source in range(lax.axis_size(axis))]
    return lax.ppermute(value, axis, pairs)


def from_behind(x, axis, by):
    size = lax.axis_size(axis)
    return lax.ppermute(x, axis, [(i, (i + by) % size) for i in range(size)])


def from_behind_2(x, axis, by):
    size = lax.axis_size(axis)
    pairs = [(i, i + by) for i in range(size) if 0 <= i + by < size]
    return lax.ppermute(x, axis, pairs)


def layer_norm(activity, gain_vec):
    centred = activity - jnp.mean(activity, axis=-1, keepdims=True)
    spread = jnp.mean(centred * centred, axis=-1, keepdims=True)
    return centred * lax.rsqrt(spread + NORM_EPS) * gain_vec


def gelu_tanh(activity):
    return jax.nn.gelu(activity, approximate=True)


def to_windows(tokens_in):
    levels_n, rows_n, cols_n, chans = tokens_in.shape
    shaped = tokens_in.reshape(
        levels_n // WIN_LEVELS,
        WIN_LEVELS,
        rows_n // WIN_LAT,
        WIN_LAT,
        cols_n // WIN_LON,
        WIN_LON,
        chans,
    )
    shaped = shaped.transpose(0, 2, 4, 1, 3, 5, 6)
    return shaped.reshape(
        levels_n // WIN_LEVELS, rows_n // WIN_LAT, cols_n // WIN_LON, WIN_TOKENS, chans
    )


def from_windows(blocks_in):
    level_w, lat_w, lon_w, _, chans = blocks_in.shape
    shaped = blocks_in.reshape(level_w, lat_w, lon_w, WIN_LEVELS, WIN_LAT, WIN_LON, chans)
    shaped = shaped.transpose(0, 3, 1, 4, 2, 5, 6)
    return shaped.reshape(level_w * WIN_LEVELS, lat_w * WIN_LAT, lon_w * WIN_LON, chans)


def pair_map():
    offsets = 2 * WIN_LON - 1
    group_count = WIN_LEVELS * WIN_LAT
    inner = jnp.arange(group_count * offsets, dtype=jnp.int32)
    inner_group = inner // offsets
    inner_off = inner % offsets
    keys_all = jnp.arange(WIN_TOKENS, dtype=jnp.int32)
    key_group = keys_all // WIN_LON
    key_col = keys_all % WIN_LON
    query_col = jnp.arange(WIN_LON, dtype=jnp.int32)
    same_group = inner_group[:, None, None] == key_group[None, None, :]
    same_off = (
        inner_off[:, None, None] == query_col[None, :, None] - key_col[None, None, :] + WIN_LON - 1
    )
    table = jnp.logical_and(same_group, same_off).astype(jnp.float32)
    return table.reshape(group_count * offsets, WIN_LON * WIN_TOKENS)


def region(position, extent, window_len):
    return jnp.where(
        position < extent - window_len, 0, jnp.where(position < extent - window_len // 2, 1, 2)
    ).astype(jnp.int32)


def dense_bias(table_rows, spread_map, first_row, lat_total, shifted):
    leading = table_rows.shape[:-1]
    group_count = WIN_LEVELS * WIN_LAT
    rows = table_rows.reshape(
        leading + (WIN_LEVELS, WIN_LEVELS, WIN_LAT, WIN_LAT * (2 * WIN_LON - 1))
    )
    rows = jnp.swapaxes(rows, -3, -2)
    rows = rows.reshape(leading + (group_count, group_count * (2 * WIN_LON - 1)))
    spread = jnp.einsum("...rg,gm->...rm", rows, spread_map, precision=lax.Precision.HIGHEST)
    bias_dense = spread.reshape(leading + (WIN_TOKENS, WIN_TOKENS))
    if shifted:
        local_rows = table_rows.shape[1] * WIN_LAT
        level_ids = region(jnp.arange(LEVELS, dtype=jnp.int32), LEVELS, WIN_LEVELS)
        row_ids = region(first_row + jnp.arange(local_rows, dtype=jnp.int32), lat_total, WIN_LAT)
        region_ids = level_ids[:, None] * 3 + row_ids[None, :]
        region_grid = jnp.broadcast_to(
            region_ids[:, :, None, None], (LEVELS, local_rows, WIN_LON, 1)
        )
        token_ids = to_windows(region_grid)[:, :, 0, :, 0]
        matched = token_ids[..., :, None] == token_ids[..., None, :]
        bias_dense = bias_dense + jnp.where(matched, 0.0, MASK_FILL).astype(jnp.float32)[:, :, None]
    return bias_dense[:, :, None]


def mix_tokens(tokens_in, weight):
    token_rows = tokens_in.reshape(-1, tokens_in.shape[-1])
    result = jnp.dot(token_rows, weight, preferred_element_type=jnp.float32)
    return result.reshape(tokens_in.shape[:-1] + (weight.shape[1],))


def mix_back(tokens_in, weight):
    token_rows = tokens_in.reshape(-1, tokens_in.shape[-1])
    result = lax.dot_general(
        token_rows, weight, (((1,), (1,)), ((), ())), preferred_element_type=jnp.float32
    )
    return result.reshape(tokens_in.shape[:-1] + (weight.shape[0],))


def grad_weight(tokens_in, grad_in):
    token_rows = tokens_in.reshape(-1, tokens_in.shape[-1])
    grad_rows = grad_in.reshape(-1, grad_in.shape[-1])
    return lax.dot_general(
        token_rows, grad_rows, (((0,), (0,)), ((), ())), preferred_element_type=jnp.float32
    )


def table_grad(grad_scores, spread_map):
    summed = jnp.sum(grad_scores, axis=2)
    leading = summed.shape[:3]
    group_count = WIN_LEVELS * WIN_LAT
    shaped = summed.reshape(leading + (group_count, WIN_LON * WIN_TOKENS))
    folded = jnp.einsum("...rm,gm->...rg", shaped, spread_map, precision=lax.Precision.HIGHEST)
    folded = folded.reshape(
        leading + (WIN_LEVELS, WIN_LAT, WIN_LEVELS, WIN_LAT * (2 * WIN_LON - 1))
    )
    folded = jnp.swapaxes(folded, -3, -2)
    return folded.reshape(leading + (BIAS_SLOTS,))


def token_major(head_major):
    leading = head_major.shape[:-3]
    merged = head_major.reshape(
        leading + (head_major.shape[-3] * head_major.shape[-2], head_major.shape[-1])
    )
    return jnp.swapaxes(merged, -1, -2)


def attend_forward(windows, bias_dense, input_weight, output_weight):
    leading = windows.shape[:-2]
    token_rows = windows.reshape(-1, MODEL_WIDTH)
    projected = jnp.dot(token_rows, input_weight, preferred_element_type=jnp.float32)
    column_scale = jnp.where(
        jnp.arange(3 * MODEL_WIDTH) < MODEL_WIDTH, HEAD_SIZE ** (-0.5), 1.0
    ).astype(jnp.float32)
    projected_b = (projected * column_scale).astype(jnp.bfloat16)
    heads_all = jnp.swapaxes(projected_b.reshape(leading + (WIN_TOKENS, 3 * MODEL_WIDTH)), -1, -2)
    heads_all = heads_all.reshape(leading + (3, HEADS, HEAD_SIZE, WIN_TOKENS))
    queries = heads_all[..., 0, :, :, :]
    key_part = heads_all[..., 1, :, :, :]
    values = heads_all[..., 2, :, :, :]
    scores = (
        jnp.einsum("...heq,...hek->...hqk", queries, key_part, preferred_element_type=jnp.float32)
        + bias_dense
    )
    attention = jax.nn.softmax(scores, axis=-1)
    weights = attention.astype(jnp.bfloat16)
    mixture_heads = jnp.einsum(
        "...hqk,...hek->...heq", weights, values, preferred_element_type=jnp.float32
    ).astype(jnp.bfloat16)
    mixture = token_major(mixture_heads)
    attended = jnp.dot(
        mixture.reshape(-1, MODEL_WIDTH), output_weight, preferred_element_type=jnp.float32
    )
    return (
        attended.reshape(windows.shape),
        (token_rows, queries, key_part, values, attention, weights, mixture),
    )


def attend_backward(saved, grad_windows_in, input_weight, output_weight):
    token_rows, queries, key_part, values, attention, weights, mixture = saved
    leading = grad_windows_in.shape[:-2]
    grad_rows = grad_windows_in.reshape(-1, MODEL_WIDTH)
    output_grad = grad_weight(mixture.reshape(-1, MODEL_WIDTH), grad_rows)
    grad_mixture = (
        mix_back(grad_rows, output_weight)
        .astype(jnp.bfloat16)
        .reshape(leading + (WIN_TOKENS, MODEL_WIDTH))
    )
    grad_mixture = jnp.swapaxes(grad_mixture, -1, -2).reshape(
        leading + (HEADS, HEAD_SIZE, WIN_TOKENS)
    )
    grad_values = jnp.einsum(
        "...hqk,...heq->...hek", weights, grad_mixture, preferred_element_type=jnp.float32
    )
    grad_weights = jnp.einsum(
        "...heq,...hek->...hqk", grad_mixture, values, preferred_element_type=jnp.float32
    )
    grad_scores = attention * (
        grad_weights - jnp.sum(attention * grad_weights, axis=-1, keepdims=True)
    )
    score_part = grad_scores.astype(jnp.bfloat16)
    grad_queries = jnp.einsum(
        "...hqk,...hek->...heq", score_part, key_part, preferred_element_type=jnp.float32
    ) * HEAD_SIZE ** (-0.5)
    grad_keys = jnp.einsum(
        "...hqk,...heq->...hek", score_part, queries, preferred_element_type=jnp.float32
    )
    grad_heads = jnp.stack([grad_queries, grad_keys, grad_values], axis=-4).astype(jnp.bfloat16)
    grad_projected = token_major(
        grad_heads.reshape(leading + (3 * HEADS, HEAD_SIZE, WIN_TOKENS))
    ).reshape(-1, 3 * MODEL_WIDTH)
    input_grad = grad_weight(token_rows, grad_projected)
    grad_windows = mix_back(grad_projected, input_weight).reshape(grad_windows_in.shape)
    return (grad_windows, input_grad, output_grad, grad_scores)


def lat_trade(edge_rows):
    return swapped(edge_rows, "lat", 0)


def roll_fore(tokens_in):
    half_rows = WIN_LAT // 2
    half_cols = WIN_LON // 2
    moved = jnp.roll(tokens_in, -(WIN_LEVELS // 2), axis=0)
    incoming = lat_trade(moved[:, :half_rows])
    moved = jnp.concatenate([moved[:, half_rows:], incoming], axis=1)
    incoming = from_behind(moved[:, :, :half_cols], "lon", -1)
    return jnp.concatenate([moved[:, :, half_cols:], incoming], axis=2)


def roll_back(tokens_in):
    half_rows = WIN_LAT // 2
    half_cols = WIN_LON // 2
    moved = jnp.roll(tokens_in, WIN_LEVELS // 2, axis=0)
    incoming = from_behind(moved[:, :, -half_cols:], "lon", 1)
    moved = jnp.concatenate([incoming, moved[:, :, :-half_cols]], axis=2)
    incoming = lat_trade(moved[:, -half_rows:])
    return jnp.concatenate([incoming, moved[:, :-half_rows]], axis=1)


def block_forward(
    block_in,
    gain_pair,
    input_weight,
    output_weight,
    expand_weight,
    reduce_weight,
    bias_dense,
    shifted,
):
    block_f = block_in.astype(jnp.float32)
    normed, norm_back = jax.vjp(layer_norm, block_f, gain_pair[0])
    normed_b = normed.astype(jnp.bfloat16)
    framed = roll_fore(normed_b) if shifted else normed_b
    attended, attn_saved = attend_forward(
        to_windows(framed), bias_dense, input_weight, output_weight
    )
    attended = from_windows(attended)
    if shifted:
        attended = roll_back(attended.astype(jnp.bfloat16)).astype(jnp.float32)
    middle = (block_f + attended).astype(jnp.bfloat16)
    middle_f = middle.astype(jnp.float32)
    normed_mid, mid_back = jax.vjp(layer_norm, middle_f, gain_pair[1])
    normed_mid_b = normed_mid.astype(jnp.bfloat16)
    hidden, gelu_back = jax.vjp(gelu_tanh, mix_tokens(normed_mid_b, expand_weight))
    hidden_b = hidden.astype(jnp.bfloat16)
    output = (middle_f + mix_tokens(hidden_b, reduce_weight)).astype(jnp.bfloat16)
    return (output, (norm_back, attn_saved, mid_back, normed_mid_b, gelu_back, hidden_b))


def block_backward(
    saved, grad_in, input_weight, output_weight, expand_weight, reduce_weight, spread_map, shifted
):
    norm_back, attn_saved, mid_back, normed_mid_b, gelu_back, hidden_b = saved
    reduce_grad = grad_weight(hidden_b, grad_in)
    grad_pre = gelu_back(mix_back(grad_in, reduce_weight))[0].astype(jnp.bfloat16)
    expand_grad = grad_weight(normed_mid_b, grad_pre)
    grad_mid_norm, gain_mid_grad = mid_back(mix_back(grad_pre, expand_weight))
    grad_middle = grad_in.astype(jnp.float32) + grad_mid_norm
    grad_middle_b = grad_middle.astype(jnp.bfloat16)
    grad_attended = roll_fore(grad_middle_b) if shifted else grad_middle_b
    grad_windows, input_grad, output_grad, grad_scores = attend_backward(
        attn_saved, to_windows(grad_attended), input_weight, output_weight
    )
    grad_normed = from_windows(grad_windows).astype(jnp.bfloat16)
    if shifted:
        grad_normed = roll_back(grad_normed)
    grad_in_norm, gain_in_grad = norm_back(grad_normed.astype(jnp.float32))
    grad_out = (grad_middle + grad_in_norm).astype(jnp.bfloat16)
    return (
        grad_out,
        (
            input_grad,
            output_grad,
            expand_grad,
            reduce_grad,
            jnp.stack([gain_in_grad, gain_mid_grad]),
            table_grad(grad_scores, spread_map),
        ),
    )


def on_device(
    inputs,
    grad_output,
    norm_gains,
    input_weight,
    output_weight,
    expand_weight,
    reduce_weight,
    bias_table,
):
    lat_index = lax.axis_index("lat")
    window_rows = LAT_DEV // WIN_LAT
    lat_total = LAT_DEV * lax.axis_size("lat")
    first_row = lat_index * LAT_DEV
    first_window = lat_index * window_rows
    spread_map = pair_map()
    savings = []
    block_in = inputs[0]
    for block in range(BLOCKS):
        table_rows = lax.dynamic_slice_in_dim(
            bias_table[0, block], first_window, window_rows, axis=1
        )
        bias_dense = dense_bias(table_rows, spread_map, first_row, lat_total, block % 2 == 1)
        block_in, saved = block_forward(
            block_in,
            norm_gains[0, block],
            input_weight[0, block],
            output_weight[0, block],
            expand_weight[0, block],
            reduce_weight[0, block],
            bias_dense,
            block % 2 == 1,
        )
        savings.append(saved)
    grad_flow = grad_output[0]
    collected = [None] * BLOCKS
    for block in reversed(range(BLOCKS)):
        grad_flow, collected[block] = block_backward(
            savings[block],
            grad_flow,
            input_weight[0, block],
            output_weight[0, block],
            expand_weight[0, block],
            reduce_weight[0, block],
            spread_map,
            block % 2 == 1,
        )
    stacked = [
        jnp.stack([collected[block][index] for block in range(BLOCKS)]) for index in range(6)
    ]
    full_table = lax.dynamic_update_slice_in_dim(
        jnp.zeros(bias_table.shape[1:], jnp.float32), stacked[5], first_window, axis=2
    )
    summed = lax.psum(
        (stacked[0], stacked[1], stacked[2], stacked[3], stacked[4], full_table), ("lon", "lat")
    )
    weight_sums = summed[:5]
    table_out = summed[5]
    grad_scale = float(LEVELS * lat_total * LON_DEV * lax.axis_size("lon")) ** (-0.5)
    upstream = from_behind_2(grad_flow, "section", -1)
    return (
        upstream[None],
        (weight_sums[0] * grad_scale)[None],
        (weight_sums[1] * grad_scale)[None],
        (weight_sums[2] * grad_scale)[None],
        (weight_sums[3] * grad_scale)[None],
        (weight_sums[4] * grad_scale)[None],
        table_out[None],
    )


def solution(mesh):
    return jax.shard_map(
        on_device,
        mesh=mesh,
        in_specs=(
            P("section", None, "lat", "lon", None),
            P("section", None, "lat", "lon", None),
            P("section", None, None, None),
            P("section", None, None, None),
            P("section", None, None, None),
            P("section", None, None, None),
            P("section", None, None, None),
            P("section", None, None, None, None, None),
        ),
        out_specs=(
            P("section", None, "lat", "lon", None),
            P("section", None, None, None),
            P("section", None, None, None),
            P("section", None, None, None),
            P("section", None, None, None),
            P("section", None, None, None),
            P("section", None, None, None, None, None),
        ),
        check_vma=False,
    )
```

profile of v0, /device:TPU:8, one launch (start us, length us, event | category | flops | bytes accessed | tf_op | source)
XLA Modules:
  0.0 966.2 jit_solution(9818680379104815907)
XLA Ops:
  12.6 1.4 multiply_convert_fusion.3
  14.0 1.4 copy.82
  15.5 2.0 compare_and_fusion
  17.5 3.8 copy.88
  21.4 1.6 fusion.148
  23.0 1.4 constant_dynamic-slice_fusion
  26.1 3.9 fusion.156
  29.9 3.5 broadcast_in_dim_reshape.3
  33.4 3.5 copy.91
  37.0 2.9 convolution_add_fusion
  39.9 3.4 fusion.152
  43.4 2.7 convolution_convert_fusion.8
  47.4 1.4 fusion.153
  53.9 2.3 collective-permute-start
  58.5 1.3 reshape.891
  59.8 3.6 fusion.157
  65.1 2.0 fusion.120
  67.1 8.1 collective-permute-start.1
  76.1 3.4 reshape.859
  79.5 5.6 copy.102
  87.8 3.1 add_add_fusion
  90.9 2.9 fusion.155
  93.9 4.2 convolution_convert_fusion.7
  99.2 9.4 collective-permute-done.2
  108.8 1.3 collective-permute-start.3
  110.1 4.1 reshape.888
  114.5 1.6 collective-permute-done.3
  116.7 2.0 multiply_convert_fusion
  118.8 1.7 fusion.19
  122.5 1.3 collective-permute-start.4
  123.8 1.5 convolution_bitcast_fusion.2
  125.6 4.2 collective-permute-done.4
  131.4 4.4 collective-permute-done.5
  137.5 5.0 fusion.40
  142.5 2.0 multiply_reduce_fusion.1
  146.0 1.4 fusion.39
  148.7 3.4 copy.124
  152.0 1.5 pad_maximum_fusion
  154.9 2.3 dot_general.151
  157.3 1.7 convolution_convert_fusion.3
  160.4 3.5 reshape.889
  163.9 5.9 fusion.27
  172.9 7.7 collective-permute-done.6
  180.8 1.3 collective-permute-start.7
  183.1 5.0 collective-permute-done.7
  190.8 1.8 convolution_bitcast_fusion.1
  192.6 1.7 fusion.12
  194.4 1.6 convolution_bitcast_fusion.3
  200.0 5.0 fusion.42
  205.0 2.0 multiply_reduce_fusion
  208.5 1.4 fusion.41
  211.1 3.4 copy.122
  214.5 2.0 convolution_bitcast_fusion.7
  216.5 4.3 reshape.887
  220.8 6.0 fusion.22
  226.8 1.6 reshape.894
  231.9 2.2 pad_maximum_fusion.3
  236.4 4.8 dynamic_update_slice.4
  241.2 2.4 pad_maximum_fusion.4
  246.7 1.9 collective-permute-start.8
  248.7 178.0 %psum.46 = f32[2,2,192]{2,1,0:T(2,128)S(1)} all-reduce(f32[2,2,192]{2,1,0:T(2,128)S(1)} %pad_maximum_fusion.15), channel_id=1, replica_groups=mesh['section'=4,'lon'=32,'lat'=2] {'lon','lat'}, use_global_device_ids=true, to_apply=%region_30.31 | all-reduce | flops 768 | bytes 6144 | tf_op jit(solution)/shard_map/psum | solution.py:375
  428.2 523.3 %all-reduce.3.cloned.1.call-done = (f32[2,192,576]{2,1,0:T(8,128)}, f32[2,192,192]{2,1,0:T(8,128)}, f32[2,192,768]{2,1,0:T(8,128)}, f32[2,768,192]{1,2,0:T(8,128)}, f32[1,2,4,2,6,3312]{5,3,4,2,1,0:T(2,128)}) async-done(((f32[2,192,576]{2,1,0:T(8,128)}, f32[2,192,192]{2,1,0:T(8,128)}, f32[2,192,768]{2,1,0:T(8,128)}, f32[2,768,192]{1,2,0:T(8,128)}, f32[1,2,4,2,6,3312]{5,3,4,2,1,0:T(2,128)}), ...) | async-done | bytes 4810768 | tf_op jit(solution)/shard_map/psum | solution.py:375
  951.5 2.4 multiply_bitcast_fusion.2
  953.9 1.8 multiply_bitcast_fusion.3
  (354 shorter events, 60.4 us)
Async XLA Ops:
  7.2 944.3 %all-reduce.3.cloned.1.call-start = ((), (), s32[]{:S(2)}) async-start(), calls=%async_computation | async-start | bytes 10027008 | tf_op jit(solution)/shard_map/psum | solution.py:375
  7.3 8.1 copy-start.102
  8.1 41.1 %copy-start.99 = (f32[1,1,1,192]{3,2,1,0:T(1,128)}, f32[1,1,1,192]{3,2,1,0:T(1,128)S(1)}, u32[]{:S(2)}) copy-start(f32[1,1,1,192]{3,2,1,0:T(1,128)S(1)} %get-tuple-element.60) | copy-start | bytes 2308
  12.6 2.9 copy-start.51
  17.5 6.9 copy-start.12
  21.4 4.7 copy-start.24
  39.9 3.4 copy-start.3
  46.1 3.8 copy-start.91
  48.8 2.7 copy-start.9
  51.8 64.3 %copy-start = (f32[8,6,12,192]{3,2,1,0:T(8,128)}, f32[8,6,12,192]{3,2,1,0:T(8,128)S(1)}, u32[]{:S(2)}) copy-start(f32[8,6,12,192]{3,2,1,0:T(8,128)S(1)} %get-tuple-element.68) | copy-start | bytes 1327108
  51.8 5.5 copy-start.46
  53.9 11.1 %collective-permute-start = (bf16[8,3,12,192]{3,2,1,0:T(8,128)(2,1)}, bf16[8,3,12,192]{3,2,1,0:T(8,128)(2,1)}, u32[]{:S(2)}, u32[]{:S(2)}) collective-permute-start(bf16[8,3,12,192]{3,2,1,0:T(8,128)(2,1)} %get-tuple-element.58), channel_id=1, source_target_pairs={{0,1},{1,0},{2,3},{3,2},{4,5},{5,4},{6,7},{7,6},{8,9},{9,8},{10,11... | collective-permute-start | bytes 331784 | tf_op jit(solution)/shard_map/ppermute | solution.py:27
  59.8 3.6 copy-start.104
  59.8 3.7 copy-start.105
  67.1 18.1 %collective-permute-start.1 = (bf16[8,6,6,192]{3,2,1,0:T(8,128)(2,1)}, bf16[8,6,6,192]{3,2,1,0:T(8,128)(2,1)}, u32[]{:S(2)}, u32[]{:S(2)}) collective-permute-start(bf16[8,6,6,192]{3,2,1,0:T(8,128)(2,1)} %get-tuple-element.56), channel_id=1, source_target_pairs={{0,62},{2,0},{4,2},{6,4},{8,6},{10,8},{12,10},{14,12},{16,14},{18,... | collective-permute-start | bytes 331784 | tf_op jit(solution)/shard_map/ppermute | solution.py:32
  79.5 5.7 copy-start.64
  79.5 6.9 copy-start.97
  79.5 7.0 copy-start.103
  85.1 2.6 copy-start.37
  87.8 6.1 copy-start.21
  90.9 3.0 copy-start.4
  93.8 4.2 copy-start.95
  93.8 4.5 copy-start.59
  98.3 11.9 %copy-start.13 = (pred[276,12,144]{2,1,0:T(8,128)(4,1)S(1)}, pred[276,12,144]{2,1,0:T(8,128)(4,1)}, u32[]{:S(2)}) copy-start(pred[276,12,144]{2,1,0:T(8,128)(4,1)} %copy-done.12) | copy-start | bytes 1430788
  99.0 15.3 %copy-start.29 = (bf16[1,8,6,12,192]{4,1,3,2,0:T(8,128)(2,1)S(1)}, bf16[1,8,6,12,192]{4,1,3,2,0:T(8,128)(2,1)}, u32[]{:S(2)}) copy-start(bf16[1,8,6,12,192]{4,1,3,2,0:T(8,128)(2,1)} %param.9) | copy-start | bytes 663556
  99.1 9.5 collective-permute-start.2
  108.8 7.3 collective-permute-start.3
  116.3 7.5 copy-start.14
  116.3 7.5 copy-start.55
  116.7 7.1 copy-start.69
  122.5 7.3 collective-permute-start.4
  125.6 10.5 %copy-start.60 = (bf16[1,2,192,192]{3,2,1,0:T(8,128)(2,1)S(1)}, bf16[1,2,192,192]{3,2,1,0:T(8,128)(2,1)}, u32[]{:S(2)}) copy-start(bf16[1,2,192,192]{3,2,1,0:T(8,128)(2,1)} %param.12) | copy-start | bytes 442372
  129.9 5.9 collective-permute-start.5
  137.5 5.0 copy-start.7
  154.9 5.5 copy-start.2
  163.9 7.3 copy-start.28
  163.9 7.3 copy-start.77
  170.3 11.9 %copy-start.32 = (bf16[576,192]{1,0:T(8,128)(2,1)S(1)}, bf16[576,192]{1,0:T(8,128)(2,1)}, u32[]{:S(2)}) copy-start(bf16[576,192]{1,0:T(8,128)(2,1)} %copy-done.31) | copy-start | bytes 663556
  170.3 11.9 %copy-start.36 = (bf16[4,1,1,192,144]{3,4,0,2,1:T(8,128)(2,1)S(1)}, bf16[4,1,1,192,144]{3,4,0,2,1:T(8,128)(2,1)}, u32[]{:S(2)}) copy-start(bf16[4,1,1,192,144]{3,4,0,2,1:T(8,128)(2,1)} %copy-done.35) | copy-start | bytes 663556
  171.2 16.9 %copy-start.1 = (f32[8,6,12,192]{3,2,1,0:T(8,128)S(1)}, f32[8,6,12,192]{3,2,1,0:T(8,128)}, u32[]{:S(2)}) copy-start(f32[8,6,12,192]{3,2,1,0:T(8,128)} %copy-done) | copy-start | bytes 1327108
  171.2 16.9 %copy-start.48 = (f32[8,6,12]{2,1,0:T(8,128)S(1)}, f32[8,6,12]{2,1,0:T(8,128)}, u32[]{:S(2)}) copy-start(f32[8,6,12]{2,1,0:T(8,128)} %copy-done.47) | copy-start | bytes 6916
  171.3 9.3 collective-permute-start.6
  171.6 16.9 %copy-start.90 = (f32[8,6,12]{2,1,0:T(8,128)S(1)}, f32[8,6,12]{2,1,0:T(8,128)}, u32[]{:S(2)}) copy-start(f32[8,6,12]{2,1,0:T(8,128)} %copy-done.89) | copy-start | bytes 6916
  171.6 16.9 %copy-start.76 = (f32[8,6,12]{2,1,0:T(8,128)S(1)}, f32[8,6,12]{2,1,0:T(8,128)}, u32[]{:S(2)}) copy-start(f32[8,6,12]{2,1,0:T(8,128)} %copy-done.75) | copy-start | bytes 6916
  180.7 8.9 copy-start.15
  180.7 8.8 copy-start.17
  180.7 8.8 copy-start.30
  180.8 8.8 copy-start.56
  180.8 8.8 copy-start.68
  180.8 8.8 copy-start.70
  180.8 8.8 copy-start.82
  180.8 7.3 collective-permute-start.7
  190.8 6.6 copy-start.26
  200.0 5.0 copy-start.5
  220.8 7.8 copy-start.44
  230.5 3.6 copy-start.65
  230.5 3.6 copy-start.66
  231.9 3.3 copy-start.62
  231.9 3.3 copy-start.63
  234.1 7.0 copy-start.41
  245.3 3.3 copy-start.101
  246.7 180.6 %collective-permute-start.8 = (bf16[8,6,12,192]{3,2,1,0:T(8,128)(2,1)S(1)}, bf16[8,6,12,192]{3,2,1,0:T(8,128)(2,1)S(1)}, u32[]{:S(2)}, u32[]{:S(2)}) collective-permute-start(bf16[8,6,12,192]{3,2,1,0:T(8,128)(2,1)S(1)} %add_convert_fusion), channel_id=1, source_target_pairs={{64,0},{128,64},{192,128},{65,1},{129,65},{193,129},{66,2},{130,66... | collective-permute-start | bytes 663560 | tf_op jit(solution)/shard_map/ppermute | solution.py:38
  951.5 4.2 copy-start.50
  951.5 5.3 copy-start.49
  (55 other events, 83.4 us)
Sparse Core Ops, SparseCore 0:
  243.7 707.7 all-reduce.2
where the time goes:
time: 974 us; the launch traced here: 966 us
  waiting for transfers between devices  556 us (57%)
  blocking collectives  178 us (18%)
  local copies, waits for them, and re-layouts  78.4 us (8%)
  matrix products  77.8 us (8%)
  other arithmetic  43.3 us (4%)
  starting transfers between devices  16.9 us (2%)
  between operations  16.2 us (2%)
    psum x1, waiting for transfers between devices, on_device(): lax.psum((stacked[0], stacked[1], stacked[2], stacked[3], stacked[4], ful...  523 us
    psum x1, blocking collectives, on_device(): lax.psum((stacked[0], stacked[1], stacked[2], stacked[3], stacked[4], ful...  178 us
    ppermute x4, waiting for transfers between devices, from_behind(): return lax.ppermute(x, axis, [(i, (i + by) % size) for i in range(size)])  21.5 us
  transfers between devices with their start and end apart: 10, of which 7 were waited for; matrix products, arithmetic and copies ran while one was open for 3% of the time, Pallas kernels for 0%

commit v1 on v0

--- a/solution.py
+++ b/solution.py
@@ -369,25 +369,39 @@
     stacked = [
         jnp.stack([collected[block][index] for block in range(BLOCKS)]) for index in range(6)
     ]
-    full_table = lax.dynamic_update_slice_in_dim(
-        jnp.zeros(bias_table.shape[1:], jnp.float32), stacked[5], first_window, axis=2
-    )
-    summed = lax.psum(
-        (stacked[0], stacked[1], stacked[2], stacked[3], stacked[4], full_table), ("lon", "lat")
-    )
-    weight_sums = summed[:5]
-    table_out = summed[5]
     grad_scale = float(LEVELS * lat_total * LON_DEV * lax.axis_size("lon")) ** (-0.5)
+    sums = reduce_grads(stacked)
     upstream = from_behind_2(grad_flow, "section", -1)
-    return (
-        upstream[None],
-        (weight_sums[0] * grad_scale)[None],
-        (weight_sums[1] * grad_scale)[None],
-        (weight_sums[2] * grad_scale)[None],
-        (weight_sums[3] * grad_scale)[None],
-        (weight_sums[4] * grad_scale)[None],
-        table_out[None],
-    )
+    return (upstream[None],) + tuple(
+        (total * grad_scale)[None] for total in sums[:5]
+    ) + (sums[5][None],)
+
+
+def reduce_grads(stacked):
+    ring = lax.axis_size("lon")
+    shapes = [piece.shape for piece in stacked]
+    sizes = [piece.size for piece in stacked]
+    flat = jnp.concatenate([piece.reshape(-1).astype(jnp.bfloat16) for piece in stacked])
+    total = flat.size
+    chunk = -(-total // (ring * 2048)) * 2048
+    flat = jnp.pad(flat, (0, chunk * ring - total)).reshape(ring, chunk // 128, 128)
+    spread = lax.all_to_all(flat, "lon", split_axis=0, concat_axis=0, tiled=True)
+    mine = jnp.sum(spread.astype(jnp.float32), axis=0).astype(jnp.bfloat16)
+    other = lat_trade(mine)
+    is_first = lax.axis_index("lat") == 0
+    pair = jnp.stack([jnp.where(is_first, mine, other), jnp.where(is_first, other, mine)])
+    pair = jnp.broadcast_to(pair[None], (ring,) + pair.shape)
+    whole = lax.all_to_all(pair, "lon", split_axis=0, concat_axis=0, tiled=True)
+    halves = whole.swapaxes(0, 1).reshape(2, -1)[:, :total].astype(jnp.float32)
+    both = halves[0] + halves[1]
+    results = []
+    offset = 0
+    for index in range(5):
+        results.append(both[offset : offset + sizes[index]].reshape(shapes[index]))
+        offset += sizes[index]
+    tables = halves[:, offset : offset + sizes[5]].reshape((2,) + shapes[5])
+    results.append(jnp.concatenate([tables[0], tables[1]], axis=2))
+    return results
 
 
 def solution(mesh):

time: 974 us -> 497 us (0.51)
  waiting for transfers between devices: 556 us -> 121 us
  blocking collectives: 178 us -> 46.9 us
  local copies, waits for them, and re-layouts: 78.4 us -> 148 us
  other arithmetic: 43.3 us -> 67.1 us
  between operations: 16.2 us -> 2.97 us
    psum x1 -> x0, waiting for transfers between devices: 523 us -> none  [on_device(): lax.psum((stacked[0], stacked[1], stacked[2], stacked[3], stacked[4], ful...]
    psum x1 -> x0, blocking collectives: 178 us -> none  [on_device(): lax.psum((stacked[0], stacked[1], stacked[2], stacked[3], stacked[4], ful...]
    all_to_all x0 -> x1, waiting for transfers between devices: none -> 79.1 us  [reduce_grads(): whole = lax.all_to_all(pair, 'lon', split_axis=0, concat_axis=0, tiled=True)]
    all_to_all x0 -> x1, blocking collectives: none -> 46.9 us  [reduce_grads(): lax.all_to_all(flat, 'lon', split_axis=0, concat_axis=0, tiled=True)]
    unnamed x221 -> x220, local copies, waits for them, and re-layouts: 8.72 us -> 49.5 us
    mul x0 -> x4, other arithmetic: none -> 22.5 us  [on_device(): total * grad_scale]
  transfers between devices with their start and end apart: 10 -> 11, of which waited for: 7 -> 9; matrix products, arithmetic and copies ran while one was open for 3% -> 6% of each run, Pallas kernels for 0% -> 0%
where the time goes in v1:
time: 497 us; the launch traced here: 488 us
  local copies, waits for them, and re-layouts  148 us (30%)
  waiting for transfers between devices  121 us (24%)
  matrix products  77.1 us (16%)
  other arithmetic  67.1 us (14%)
  blocking collectives  46.9 us (9%)
  starting transfers between devices  24.4 us (5%)
    all_to_all x1, waiting for transfers between devices, reduce_grads(): whole = lax.all_to_all(pair, 'lon', split_axis=0, concat_axis=0, tiled=True)  79.1 us
    unnamed x220, local copies, waits for them, and re-layouts  49.5 us
    all_to_all x1, blocking collectives, reduce_grads(): lax.all_to_all(flat, 'lon', split_axis=0, concat_axis=0, tiled=True)  46.9 us
    mul x4, other arithmetic, on_device(): total * grad_scale  22.5 us
    ppermute x4, waiting for transfers between devices, from_behind(): return lax.ppermute(x, axis, [(i, (i + by) % size) for i in range(size)])  21.6 us
    ppermute x5, waiting for transfers between devices, swapped(): return lax.ppermute(value, axis, pairs)  15.2 us
    dot_general x2, matrix products, table_grad(): jnp.einsum('...rm,gm->...rg', shaped, spread_map, precision=lax.Precision...  12 us
  transfers between devices with their start and end apart: 11, of which 9 were waited for; matrix products, arithmetic and copies ran while one was open for 6% of the time, Pallas kernels for 0%

profile of v1, /device:TPU:8, one launch (start us, length us, event | category | flops | bytes accessed | tf_op | source)
XLA Modules:
  0.0 487.9 jit_solution(2566727635583528830)
XLA Ops:
  9.0 2.0 compare_and_fusion
  11.0 3.8 copy.293
  14.8 1.6 fusion.174
  19.5 3.9 fusion.182
  23.4 3.5 broadcast_in_dim_reshape.3
  26.9 3.6 copy.296
  30.5 2.9 convolution_add_fusion
  33.4 3.4 fusion.178
  36.8 2.7 convolution_convert_fusion.8
  47.4 2.3 collective-permute-start
  53.3 3.6 fusion.183
  58.6 2.0 fusion.145
  60.6 8.1 %collective-permute-start.1 = (bf16[8,6,6,192]{3,2,1,0:T(8,128)(2,1)}, bf16[8,6,6,192]{3,2,1,0:T(8,128)(2,1)}, u32[]{:S(2)}, u32[]{:S(2)}) collective-permute-start(bf16[8,6,6,192]{3,2,1,0:T(8,128)(2,1)} %get-tuple-element.83), channel_id=1, source_target_pairs={{0,62},{2,0},{4,2},{6,4},{8,6},{10,8},{12,10},{14,12},{16,14},{18,... | collective-permute-start | bytes 331784 | tf_op jit(solution)/shard_map/ppermute | solution.py:32
  69.6 3.4 reshape.963
  73.0 5.7 %copy.307 = f32[4,6,144,144]{2,3,1,0:T(8,128)} copy(f32[4,6,144,144]{3,2,1,0:T(8,128)} %reshape.963) | data formatting | bytes 3981312 | tf_op jit(solution)/shard_map/reshape | solution.py:108
  81.4 3.1 add_add_fusion
  84.5 2.9 fusion.181
  87.4 4.1 convolution_convert_fusion.7
  92.4 9.4 %collective-permute-done.2 = bf16[8,6,6,192]{3,2,1,0:T(8,128)(2,1)S(1)} collective-permute-done((bf16[8,6,6,192]{3,2,1,0:T(8,128)(2,1)S(1)}, bf16[8,6,6,192]{3,2,1,0:T(8,128)(2,1)S(1)}, u32[]{:S(2)}, u32[]{:S(2)}) %collective-permute-start.2) | collective-permute-done | bytes 110624 | tf_op jit(solution)/shard_map/ppermute | solution.py:32
  103.3 4.1 reshape.992
  107.6 1.6 collective-permute-done.3
  109.9 2.0 multiply_convert_fusion
  112.0 1.7 fusion.19
  118.7 4.3 collective-permute-done.4
  124.5 4.5 collective-permute-done.5
  130.7 5.0 %fusion.43 = bf16[4,1,1,1,6,32,144]{6,5,4,0,3,2,1:T(8,128)(2,1)} fusion(bf16[4,6,32,144]{3,2,1,0:T(8,128)(2,1)} %bitcast.403, f32[4,6,144]{2,1,0:T(8,128)} %copy-done.91, f32[4,6,144,144]{2,3,1,0:T(8,128)} %copy-done.5), kind=kOutput, calls=%fused_computation.75 | convolution fusion | flops 33457680 | bytes 2446848 | tf_op jit(solution)/shard_map/...hqk,...heq->...hek/dot_general | solution.py:211
  135.7 2.0 multiply_reduce_fusion.1
  141.8 3.4 copy.330
  148.1 2.3 dot_general.151
  150.5 1.7 convolution_convert_fusion.3
  153.6 3.4 reshape.993
  157.0 6.0 %fusion.46 = bf16[4,1,6,2,2,6,138]{6,5,4,3,2,0,1:T(8,128)(2,1)S(1)} fusion(pred[2,138,1728,1,1,1]{2,1,0,3,4,5:T(8,128)(4,1)} %reshape.992, f32[4,6,2,6,1728,1]{4,3,2,1,0,5:T(8,128)} %reshape.993), kind=kOutput, calls=%fused_computation.78 | convolution fusion | flops 1648342656 | bytes 2626560 | tf_op jit(solution)/shard_map/...rm,gm->...rg/dot_general | solution.py:150
  166.1 7.8 %collective-permute-done.6 = bf16[8,6,6,192]{3,2,1,0:T(8,128)(2,1)S(1)} collective-permute-done((bf16[8,6,6,192]{3,2,1,0:T(8,128)(2,1)S(1)}, bf16[8,6,6,192]{3,2,1,0:T(8,128)(2,1)S(1)}, u32[]{:S(2)}, u32[]{:S(2)}) %collective-permute-start.6) | collective-permute-done | bytes 110624 | tf_op jit(solution)/shard_map/ppermute | solution.py:32
  176.4 5.0 %collective-permute-done.7 = bf16[8,3,12,192]{3,2,1,0:T(8,128)(2,1)S(1)} collective-permute-done((bf16[8,3,12,192]{3,2,1,0:T(8,128)(2,1)S(1)}, bf16[8,3,12,192]{3,2,1,0:T(8,128)(2,1)S(1)}, u32[]{:S(2)}, u32[]{:S(2)}) %collective-permute-start.7) | collective-permute-done | bytes 110624 | tf_op jit(solution)/shard_map/ppermute | solution.py:27
  184.0 1.7 fusion.61
  185.8 1.7 fusion.12
  193.3 5.0 %fusion.45 = bf16[4,1,1,1,6,32,144]{6,5,4,0,3,2,1:T(8,128)(2,1)} fusion(bf16[4,6,32,144]{3,2,1,0:T(8,128)(2,1)} %bitcast.405, f32[4,6,144]{2,1,0:T(8,128)} %get-tuple-element.92, f32[4,6,144,144]{2,3,1,0:T(8,128)} %copy-done.4), kind=kOutput, calls=%fused_computation.77 | convolution fusion | flops 33457680 | bytes 2446848 | tf_op jit(solution)/shard_map/...hqk,...heq->...hek/dot_general | solution.py:211
  198.3 2.0 multiply_reduce_fusion
  204.4 3.4 copy.328
  210.1 2.9 convert_element_type.230
  213.0 1.9 pad_maximum_fusion.2
  214.9 2.3 convert_element_type.228
  219.2 1.6 pad_maximum_fusion.15
  220.8 1.8 convert_element_type.227
  222.6 3.6 reshape.991
  226.2 6.0 %fusion.51 = bf16[4,1,6,2,2,6,138]{6,5,4,3,2,0,1:T(8,128)(2,1)S(1)} fusion(pred[2,138,1728,1,1,1]{2,1,0,3,4,5:T(8,128)(4,1)} %reshape.992, f32[4,6,2,6,1728,1]{4,3,2,1,0,5:T(8,128)} %reshape.991), kind=kOutput, calls=%fused_computation.79 | convolution fusion | flops 1648342656 | bytes 2626560 | tf_op jit(solution)/shard_map/...rm,gm->...rg/dot_general | solution.py:150
  245.2 2.9 dynamic-update-slice.5
  248.2 46.9 %all_to_all.10 = bf16[32,256,128]{2,1,0:T(8,128)(2,1)S(1)} all-to-all(bf16[32,256,128]{2,1,0:T(8,128)(2,1)S(1)} %bitcast.376), channel_id=1, replica_groups=mesh['section'=4,'lon'=32,'lat'=2] {'lon'}, dimensions={0} | all-to-all | bytes 4194304 | tf_op jit(solution)/shard_map/all_to_all | solution.py:388
  295.5 1.8 collective-permute-start.9
  297.3 4.3 collective-permute-done.9
  301.6 3.0 broadcast_in_dim.136
  304.7 5.5 %all-to-all-start.1 = ((bf16[32,2,256,128]{3,2,1,0:T(8,128)(2,1)}), bf16[32,2,256,128]{3,2,1,0:T(8,128)(2,1)}, u32[]{:S(2)}, u32[]{:S(2)}) async-start(bf16[32,2,256,128]{3,2,1,0:T(8,128)(2,1)} %broadcast_in_dim.136), calls=%async_computation.1 | async-start | bytes 8388608 | tf_op jit(solution)/shard_map/all_to_all | solution.py:394
  311.0 1.9 collective-permute-start.8
  312.9 5.3 %collective-permute-done.8 = bf16[8,6,12,192]{3,2,1,0:T(8,128)(2,1)S(1)} collective-permute-done((bf16[8,6,12,192]{3,2,1,0:T(8,128)(2,1)S(1)}, bf16[8,6,12,192]{3,2,1,0:T(8,128)(2,1)S(1)}, u32[]{:S(2)}, u32[]{:S(2)}) %collective-permute-start.8) | collective-permute-done | bytes 221216 | tf_op jit(solution)/shard_map/ppermute | solution.py:38
  319.1 79.1 %all-to-all-done.1 = bf16[32,2,256,128]{3,2,1,0:T(8,128)(2,1)} async-done(((bf16[32,2,256,128]{3,2,1,0:T(8,128)(2,1)}), bf16[32,2,256,128]{3,2,1,0:T(8,128)(2,1)}, u32[]{:S(2)}, u32[]{:S(2)}) %all-to-all-start.1) | async-done | bytes 4194336 | tf_op jit(solution)/shard_map/all_to_all | solution.py:394
  398.1 2.5 copy.333
  400.6 35.5 %copy.394 = bf16[1,2,8192,128]{3,1,2,0:T(2,128)(2,1)S(1)} copy(bf16[1,2,8192,128]{3,2,1,0:T(8,128)(2,1)S(1)} %bitcast.374) | data formatting | bytes 8388608
  436.1 3.0 slice_convert_fusion
  439.1 6.6 %slice_reduce_fusion.1 = (f32[158976]{0:T(1024)S(1)}, f32[158976]{0:T(1024)S(1)}) fusion(f32[2,1044480]{1,0:T(2,128)S(1)} %slice_convert_fusion), kind=kLoop, calls=%fused_computation.161 | loop fusion | bytes 2543616 | tf_op jit(solution)/shard_map/slice | solution.py:403
  445.8 4.5 slice_add_fusion
  451.8 7.3 %fusion.81 = f32[221184]{0:T(1024)S(1)} fusion(f32[1,1044480]{1,0:T(1,128)S(1)} %slice_add_fusion), kind=kLoop, calls=%fused_computation.127 | loop fusion | flops 221184 | bytes 1769472 | tf_op jit(solution)/shard_map/mul | solution.py:376
  459.2 13.6 %fusion.58 = (f32[294912]{0:T(1024)}, f32[294912]{0:T(1024)S(1)}) fusion(f32[1,1044480]{1,0:T(1,128)S(1)} %slice_add_fusion), kind=kLoop, calls=%fused_computation.94 | loop fusion | flops 589824 | bytes 4718592 | tf_op jit(solution)/shard_map/mul | solution.py:376
  474.9 1.8 mul.534
  479.9 2.0 copy.336
  (380 shorter events, 96.4 us)
Async XLA Ops:
  0.7 8.2 %copy-start.97 = (f32[576]{0:T(1024)}, f32[576]{0:T(1024)S(1)}, u32[]{:S(2)}) copy-start(f32[576]{0:T(1024)S(1)} %fusion.164) | copy-start | bytes 6916
  1.5 41.2 %copy-start.95 = (f32[1,1,1,192]{3,2,1,0:T(1,128)}, f32[1,1,1,192]{3,2,1,0:T(1,128)S(1)}, u32[]{:S(2)}) copy-start(f32[1,1,1,192]{3,2,1,0:T(1,128)S(1)} %get-tuple-element.89) | copy-start | bytes 2308
  11.0 6.9 %copy-start.13 = (pred[276,12,144]{2,1,0:T(8,128)(4,1)}, pred[276,12,144]{2,1,0:T(8,128)(4,1)S(1)}, u32[]{:S(2)}) copy-start(pred[276,12,144]{2,1,0:T(8,128)(4,1)S(1)} %compare_and_fusion) | copy-start | bytes 1430788
  14.8 4.7 copy-start.25
  39.5 3.8 copy-start.87
  45.3 64.0 %copy-start = (f32[8,6,12,192]{3,2,1,0:T(8,128)}, f32[8,6,12,192]{3,2,1,0:T(8,128)S(1)}, u32[]{:S(2)}) copy-start(f32[8,6,12,192]{3,2,1,0:T(8,128)S(1)} %get-tuple-element.97) | copy-start | bytes 1327108
  45.3 5.5 %copy-start.36 = (f32[1,1,4,1,6,3312]{5,3,4,2,1,0:T(1,128)S(1)}, f32[1,1,4,1,6,3312]{5,3,4,2,1,0:T(1,128)}, u32[]{:S(2)}) copy-start(f32[1,1,4,1,6,3312]{5,3,4,2,1,0:T(1,128)} %get-tuple-element.111) | copy-start | bytes 953860
  47.4 11.2 %collective-permute-start = (bf16[8,3,12,192]{3,2,1,0:T(8,128)(2,1)}, bf16[8,3,12,192]{3,2,1,0:T(8,128)(2,1)}, u32[]{:S(2)}, u32[]{:S(2)}) collective-permute-start(bf16[8,3,12,192]{3,2,1,0:T(8,128)(2,1)} %get-tuple-element.85), channel_id=1, source_target_pairs={{0,1},{1,0},{2,3},{3,2},{4,5},{5,4},{6,7},{7,6},{8,9},{9,8},{10,11... | collective-permute-start | bytes 331784 | tf_op jit(solution)/shard_map/ppermute | solution.py:27
  53.3 3.6 copy-start.100
  53.3 3.7 copy-start.101
  60.6 18.1 %collective-permute-start.1 = (bf16[8,6,6,192]{3,2,1,0:T(8,128)(2,1)}, bf16[8,6,6,192]{3,2,1,0:T(8,128)(2,1)}, u32[]{:S(2)}, u32[]{:S(2)}) collective-permute-start(bf16[8,6,6,192]{3,2,1,0:T(8,128)(2,1)} %get-tuple-element.83), channel_id=1, source_target_pairs={{0,62},{2,0},{4,2},{6,4},{8,6},{10,8},{12,10},{14,12},{16,14},{18,... | collective-permute-start | bytes 331784 | tf_op jit(solution)/shard_map/ppermute | solution.py:32
  73.0 5.7 %copy-start.58 = (bf16[8,6,6,192]{3,2,1,0:T(8,128)(2,1)S(1)}, bf16[8,6,6,192]{3,2,1,0:T(8,128)(2,1)}, u32[]{:S(2)}) copy-start(bf16[8,6,6,192]{3,2,1,0:T(8,128)(2,1)} %get-tuple-element.82) | copy-start | bytes 331780
  73.0 7.0 %copy-start.94 = (bf16[1,2,192,576]{3,2,1,0:T(8,128)(2,1)S(1)}, bf16[1,2,192,576]{3,2,1,0:T(8,128)(2,1)}, u32[]{:S(2)}) copy-start(bf16[1,2,192,576]{3,2,1,0:T(8,128)(2,1)} %param.11) | copy-start | bytes 1327108
  73.0 7.0 %copy-start.98 = (f32[576]{0:T(1024)S(1)}, f32[576]{0:T(1024)}, u32[]{:S(2)}) copy-start(f32[576]{0:T(1024)} %copy-done.97) | copy-start | bytes 6916
  81.3 6.1 %copy-start.22 = (bf16[4,1,1,144,576]{3,4,0,2,1:T(8,128)(2,1)}, bf16[4,1,1,144,576]{3,4,0,2,1:T(8,128)(2,1)S(1)}, u32[]{:S(2)}) copy-start(bf16[4,1,1,144,576]{3,4,0,2,1:T(8,128)(2,1)S(1)} %copy.299) | copy-start | bytes 1990660
  87.4 4.1 copy-start.91
  87.4 4.5 copy-start.55
  91.8 10.2 %copy-start.47 = (bf16[4,1,1,192,144]{3,4,0,2,1:T(8,128)(2,1)}, bf16[4,1,1,192,144]{3,4,0,2,1:T(8,128)(2,1)S(1)}, u32[]{:S(2)}) copy-start(bf16[4,1,1,192,144]{3,4,0,2,1:T(8,128)(2,1)S(1)} %copy.309) | copy-start | bytes 663556
  91.8 11.6 %copy-start.14 = (pred[276,12,144]{2,1,0:T(8,128)(4,1)S(1)}, pred[276,12,144]{2,1,0:T(8,128)(4,1)}, u32[]{:S(2)}) copy-start(pred[276,12,144]{2,1,0:T(8,128)(4,1)} %copy-done.13) | copy-start | bytes 1430788
  92.2 15.3 %copy-start.29 = (bf16[1,8,6,12,192]{4,1,3,2,0:T(8,128)(2,1)S(1)}, bf16[1,8,6,12,192]{4,1,3,2,0:T(8,128)(2,1)}, u32[]{:S(2)}) copy-start(bf16[1,8,6,12,192]{4,1,3,2,0:T(8,128)(2,1)} %param.9) | copy-start | bytes 663556
  92.3 9.5 %collective-permute-start.2 = (bf16[8,6,6,192]{3,2,1,0:T(8,128)(2,1)S(1)}, bf16[8,6,6,192]{3,2,1,0:T(8,128)(2,1)S(1)}, u32[]{:S(2)}, u32[]{:S(2)}) collective-permute-start(bf16[8,6,6,192]{3,2,1,0:T(8,128)(2,1)S(1)} %fusion.144), channel_id=1, source_target_pairs={{0,2},{2,4},{4,6},{6,8},{8,10},{10,12},{12,14},{14,16},{16,18},{18... | collective-permute-start | bytes 331784 | tf_op jit(solution)/shard_map/ppermute | solution.py:32
  102.0 7.3 %collective-permute-start.3 = (bf16[8,3,12,192]{3,2,1,0:T(8,128)(2,1)S(1)}, bf16[8,3,12,192]{3,2,1,0:T(8,128)(2,1)S(1)}, u32[]{:S(2)}, u32[]{:S(2)}) collective-permute-start(bf16[8,3,12,192]{3,2,1,0:T(8,128)(2,1)S(1)} %get-tuple-element.80), channel_id=1, source_target_pairs={{0,1},{1,0},{2,3},{3,2},{4,5},{5,4},{6,7},{7,6},{8,9},{9,8},{10,11... | collective-permute-start | bytes 331784 | tf_op jit(solution)/shard_map/ppermute | solution.py:27
  109.5 7.5 %copy-start.15 = (bf16[8,6,12,192]{3,2,1,0:T(8,128)(2,1)}, bf16[8,6,12,192]{3,2,1,0:T(8,128)(2,1)S(1)}, u32[]{:S(2)}) copy-start(bf16[8,6,12,192]{3,2,1,0:T(8,128)(2,1)S(1)} %get-tuple-element.71) | copy-start | bytes 663556
  109.5 7.5 %copy-start.51 = (f32[8,6,12]{2,1,0:T(8,128)}, f32[8,6,12]{2,1,0:T(8,128)S(1)}, u32[]{:S(2)}) copy-start(f32[8,6,12]{2,1,0:T(8,128)S(1)} %broadcast_multiply_fusion) | copy-start | bytes 6916
  109.9 7.1 %copy-start.62 = (f32[8,6,12]{2,1,0:T(8,128)}, f32[8,6,12]{2,1,0:T(8,128)S(1)}, u32[]{:S(2)}) copy-start(f32[8,6,12]{2,1,0:T(8,128)S(1)} %fusion.158) | copy-start | bytes 6916
  115.7 7.3 %collective-permute-start.4 = (bf16[8,3,12,192]{3,2,1,0:T(8,128)(2,1)S(1)}, bf16[8,3,12,192]{3,2,1,0:T(8,128)(2,1)S(1)}, u32[]{:S(2)}, u32[]{:S(2)}) collective-permute-start(bf16[8,3,12,192]{3,2,1,0:T(8,128)(2,1)S(1)} %get-tuple-element.79), channel_id=1, source_target_pairs={{0,1},{1,0},{2,3},{3,2},{4,5},{5,4},{6,7},{7,6},{8,9},{9,8},{10,11... | collective-permute-start | bytes 331784 | tf_op jit(solution)/shard_map/ppermute | solution.py:27
  118.6 10.6 %copy-start.56 = (bf16[1,2,192,192]{3,2,1,0:T(8,128)(2,1)S(1)}, bf16[1,2,192,192]{3,2,1,0:T(8,128)(2,1)}, u32[]{:S(2)}) copy-start(bf16[1,2,192,192]{3,2,1,0:T(8,128)(2,1)} %param.12) | copy-start | bytes 442372
  123.1 5.9 %collective-permute-start.5 = (bf16[8,6,6,192]{3,2,1,0:T(8,128)(2,1)S(1)}, bf16[8,6,6,192]{3,2,1,0:T(8,128)(2,1)S(1)}, u32[]{:S(2)}, u32[]{:S(2)}) collective-permute-start(bf16[8,6,6,192]{3,2,1,0:T(8,128)(2,1)S(1)} %get-tuple-element.77), channel_id=1, source_target_pairs={{0,62},{2,0},{4,2},{6,4},{8,6},{10,8},{12,10},{14,12},{16,14},{18,... | collective-permute-start | bytes 331784 | tf_op jit(solution)/shard_map/ppermute | solution.py:32
  130.7 5.0 %copy-start.8 = (f32[4,6,144,144]{2,3,1,0:T(8,128)S(1)}, f32[4,6,144,144]{2,3,1,0:T(8,128)}, u32[]{:S(2)}) copy-start(f32[4,6,144,144]{2,3,1,0:T(8,128)} %get-tuple-element.99) | copy-start | bytes 5971972
  148.1 5.5 %copy-start.3 = (f32[4,6,144,144]{3,2,1,0:T(8,128)S(1)}, f32[4,6,144,144]{3,2,1,0:T(8,128)}, u32[]{:S(2)}) copy-start(f32[4,6,144,144]{3,2,1,0:T(8,128)} %copy.330) | copy-start | bytes 5971972
  157.0 7.3 %copy-start.28 = (bf16[7,6,12,192]{3,2,1,0:T(8,128)(2,1)S(1)}, bf16[7,6,12,192]{3,2,1,0:T(8,128)(2,1)}, u32[]{:S(2)}) copy-start(bf16[7,6,12,192]{3,2,1,0:T(8,128)(2,1)} %slice.273) | copy-start | bytes 580612
  157.0 7.3 %copy-start.71 = (bf16[1,6,12,192]{3,2,1,0:T(8,128)(2,1)S(1)}, bf16[1,6,12,192]{3,2,1,0:T(8,128)(2,1)}, u32[]{:S(2)}) copy-start(bf16[1,6,12,192]{3,2,1,0:T(8,128)(2,1)} %slice.272) | copy-start | bytes 82948
  157.0 7.9 %copy-start.21 = (bf16[4,1,1,144,576]{4,3,0,2,1:T(8,128)(2,1)S(1)}, bf16[4,1,1,144,576]{4,3,0,2,1:T(8,128)(2,1)}, u32[]{:S(2)}) copy-start(bf16[4,1,1,144,576]{4,3,0,2,1:T(8,128)(2,1)} %copy.316) | copy-start | bytes 1990660
  157.0 7.9 %copy-start.42 = (bf16[576,192]{1,0:T(8,128)(2,1)S(1)}, bf16[576,192]{1,0:T(8,128)(2,1)}, u32[]{:S(2)}) copy-start(bf16[576,192]{1,0:T(8,128)(2,1)} %copy-done.41) | copy-start | bytes 663556
  163.0 12.4 %copy-start.44 = (bf16[576,192]{1,0:T(8,128)(2,1)S(1)}, bf16[576,192]{1,0:T(8,128)(2,1)}, u32[]{:S(2)}) copy-start(bf16[576,192]{1,0:T(8,128)(2,1)} %copy-done.43) | copy-start | bytes 663556
  163.0 12.4 %copy-start.48 = (bf16[4,1,1,192,144]{3,4,0,2,1:T(8,128)(2,1)S(1)}, bf16[4,1,1,192,144]{3,4,0,2,1:T(8,128)(2,1)}, u32[]{:S(2)}) copy-start(bf16[4,1,1,192,144]{3,4,0,2,1:T(8,128)(2,1)} %copy-done.47) | copy-start | bytes 663556
  163.6 17.8 %copy-start.1 = (f32[8,6,12,192]{3,2,1,0:T(8,128)S(1)}, f32[8,6,12,192]{3,2,1,0:T(8,128)}, u32[]{:S(2)}) copy-start(f32[8,6,12,192]{3,2,1,0:T(8,128)} %copy-done) | copy-start | bytes 1327108
  163.6 17.8 %copy-start.38 = (f32[8,6,12]{2,1,0:T(8,128)S(1)}, f32[8,6,12]{2,1,0:T(8,128)}, u32[]{:S(2)}) copy-start(f32[8,6,12]{2,1,0:T(8,128)} %copy-done.37) | copy-start | bytes 6916
  164.4 9.5 %collective-permute-start.6 = (bf16[8,6,6,192]{3,2,1,0:T(8,128)(2,1)S(1)}, bf16[8,6,6,192]{3,2,1,0:T(8,128)(2,1)S(1)}, u32[]{:S(2)}, u32[]{:S(2)}) collective-permute-start(bf16[8,6,6,192]{3,2,1,0:T(8,128)(2,1)S(1)} %fusion.141), channel_id=1, source_target_pairs={{0,2},{2,4},{4,6},{6,8},{8,10},{10,12},{12,14},{14,16},{16,18},{18... | collective-permute-start | bytes 331784 | tf_op jit(solution)/shard_map/ppermute | solution.py:32
  165.0 16.8 %copy-start.86 = (f32[8,6,12]{2,1,0:T(8,128)S(1)}, f32[8,6,12]{2,1,0:T(8,128)}, u32[]{:S(2)}) copy-start(f32[8,6,12]{2,1,0:T(8,128)} %copy-done.85) | copy-start | bytes 6916
  165.0 16.8 %copy-start.70 = (f32[8,6,12]{2,1,0:T(8,128)S(1)}, f32[8,6,12]{2,1,0:T(8,128)}, u32[]{:S(2)}) copy-start(f32[8,6,12]{2,1,0:T(8,128)} %copy-done.69) | copy-start | bytes 6916
  166.1 16.7 %copy-start.16 = (bf16[8,6,12,192]{3,2,1,0:T(8,128)(2,1)S(1)}, bf16[8,6,12,192]{3,2,1,0:T(8,128)(2,1)}, u32[]{:S(2)}) copy-start(bf16[8,6,12,192]{3,2,1,0:T(8,128)(2,1)} %copy-done.15) | copy-start | bytes 663556
  166.1 16.7 %copy-start.18 = (f32[8,6,12,192]{3,2,1,0:T(8,128)S(1)}, f32[8,6,12,192]{3,2,1,0:T(8,128)}, u32[]{:S(2)}) copy-start(f32[8,6,12,192]{3,2,1,0:T(8,128)} %copy-done.17) | copy-start | bytes 1327108
  166.1 16.7 %copy-start.30 = (bf16[1,8,6,12,192]{4,1,3,2,0:T(8,128)(2,1)S(1)}, bf16[1,8,6,12,192]{4,1,3,2,0:T(8,128)(2,1)}, u32[]{:S(2)}) copy-start(bf16[1,8,6,12,192]{4,1,3,2,0:T(8,128)(2,1)} %param.9) | copy-start | bytes 663556
  166.1 16.7 %copy-start.52 = (f32[8,6,12]{2,1,0:T(8,128)S(1)}, f32[8,6,12]{2,1,0:T(8,128)}, u32[]{:S(2)}) copy-start(f32[8,6,12]{2,1,0:T(8,128)} %copy-done.51) | copy-start | bytes 6916
  166.1 16.8 %copy-start.61 = (f32[8,6,12]{2,1,0:T(8,128)S(1)}, f32[8,6,12]{2,1,0:T(8,128)}, u32[]{:S(2)}) copy-start(f32[8,6,12]{2,1,0:T(8,128)} %copy-done.60) | copy-start | bytes 6916
  166.1 16.8 %copy-start.63 = (f32[8,6,12]{2,1,0:T(8,128)S(1)}, f32[8,6,12]{2,1,0:T(8,128)}, u32[]{:S(2)}) copy-start(f32[8,6,12]{2,1,0:T(8,128)} %copy-done.62) | copy-start | bytes 6916
  166.1 16.8 %copy-start.76 = (f32[8,6,12]{2,1,0:T(8,128)S(1)}, f32[8,6,12]{2,1,0:T(8,128)}, u32[]{:S(2)}) copy-start(f32[8,6,12]{2,1,0:T(8,128)} %copy-done.75) | copy-start | bytes 6916
  174.1 7.3 %collective-permute-start.7 = (bf16[8,3,12,192]{3,2,1,0:T(8,128)(2,1)S(1)}, bf16[8,3,12,192]{3,2,1,0:T(8,128)(2,1)S(1)}, u32[]{:S(2)}, u32[]{:S(2)}) collective-permute-start(bf16[8,3,12,192]{3,2,1,0:T(8,128)(2,1)S(1)} %get-tuple-element.74), channel_id=1, source_target_pairs={{0,1},{1,0},{2,3},{3,2},{4,5},{5,4},{6,7},{7,6},{8,9},{9,8},{10,11... | collective-permute-start | bytes 331784 | tf_op jit(solution)/shard_map/ppermute | solution.py:27
  184.0 6.7 %copy-start.26 = (bf16[8,6,12,192]{3,2,1,0:T(8,128)(2,1)}, bf16[8,6,12,192]{3,2,1,0:T(8,128)(2,1)S(1)}, u32[]{:S(2)}) copy-start(bf16[8,6,12,192]{3,2,1,0:T(8,128)(2,1)S(1)} %add_convert_fusion.1) | copy-start | bytes 663556
  193.3 5.0 %copy-start.6 = (f32[4,6,144,144]{2,3,1,0:T(8,128)S(1)}, f32[4,6,144,144]{2,3,1,0:T(8,128)}, u32[]{:S(2)}) copy-start(f32[4,6,144,144]{2,3,1,0:T(8,128)} %get-tuple-element.93) | copy-start | bytes 5971972
  210.1 12.5 %copy-start.2 = (f32[4,6,144,144]{3,2,1,0:T(8,128)S(1)}, f32[4,6,144,144]{3,2,1,0:T(8,128)}, u32[]{:S(2)}) copy-start(f32[4,6,144,144]{3,2,1,0:T(8,128)} %copy.328) | copy-start | bytes 5971972
  226.2 6.6 %copy-start.34 = (bf16[4,1,1,1,6,32,144]{6,5,4,0,3,2,1:T(8,128)(2,1)S(1)}, bf16[4,1,1,1,6,32,144]{6,5,4,0,3,2,1:T(8,128)(2,1)}, u32[]{:S(2)}) copy-start(bf16[4,1,1,1,6,32,144]{6,5,4,0,3,2,1:T(8,128)(2,1)} %fusion.44) | copy-start | bytes 663556
  226.2 6.6 %copy-start.35 = (bf16[4,1,1,1,6,32,144]{6,5,4,0,3,2,1:T(8,128)(2,1)S(1)}, bf16[4,1,1,1,6,32,144]{6,5,4,0,3,2,1:T(8,128)(2,1)}, u32[]{:S(2)}) copy-start(bf16[4,1,1,1,6,32,144]{6,5,4,0,3,2,1:T(8,128)(2,1)} %fusion.56) | copy-start | bytes 663556
  226.2 6.6 %copy-start.72 = (bf16[4,1,1,1,6,32,144]{6,5,4,0,3,2,1:T(8,128)(2,1)S(1)}, bf16[4,1,1,1,6,32,144]{6,5,4,0,3,2,1:T(8,128)(2,1)}, u32[]{:S(2)}) copy-start(bf16[4,1,1,1,6,32,144]{6,5,4,0,3,2,1:T(8,128)(2,1)} %fusion.45) | copy-start | bytes 663556
  295.5 6.1 %collective-permute-start.9 = (bf16[256,128]{1,0:T(8,128)(2,1)S(1)}, bf16[256,128]{1,0:T(8,128)(2,1)S(1)}, u32[]{:S(2)}, u32[]{:S(2)}) collective-permute-start(bf16[256,128]{1,0:T(8,128)(2,1)S(1)} %reduce_sum.266), channel_id=1, source_target_pairs={{0,1},{1,0},{2,3},{3,2},{4,5},{5,4},{6,7},{7,6},{8,9},{9,8},{10,11... | collective-permute-start | bytes 196616 | tf_op jit(solution)/shard_map/ppermute | solution.py:27
  304.6 5.6 %copy-start.93 = (f32[8,6,12]{2,1,0:T(8,128)S(1)}, f32[8,6,12]{2,1,0:T(8,128)}, u32[]{:S(2)}) copy-start(f32[8,6,12]{2,1,0:T(8,128)} %get-tuple-element.67) | copy-start | bytes 6916
  304.6 5.6 %copy-start.20 = (f32[8,6,12,192]{3,2,1,0:T(8,128)S(1)}, f32[8,6,12,192]{3,2,1,0:T(8,128)}, u32[]{:S(2)}) copy-start(f32[8,6,12,192]{3,2,1,0:T(8,128)} %copy-done.19) | copy-start | bytes 1327108
  304.6 5.6 %copy-start.27 = (bf16[8,6,12,192]{3,2,1,0:T(8,128)(2,1)S(1)}, bf16[8,6,12,192]{3,2,1,0:T(8,128)(2,1)}, u32[]{:S(2)}) copy-start(bf16[8,6,12,192]{3,2,1,0:T(8,128)(2,1)} %copy-done.26) | copy-start | bytes 663556
  304.6 5.6 %copy-start.68 = (f32[8,6,12]{2,1,0:T(8,128)S(1)}, f32[8,6,12]{2,1,0:T(8,128)}, u32[]{:S(2)}) copy-start(f32[8,6,12]{2,1,0:T(8,128)} %copy-done.66) | copy-start | bytes 6916
  304.6 5.6 %copy-start.78 = (f32[8,6,12]{2,1,0:T(8,128)S(1)}, f32[8,6,12]{2,1,0:T(8,128)}, u32[]{:S(2)}) copy-start(f32[8,6,12]{2,1,0:T(8,128)} %copy-done.77) | copy-start | bytes 6916
  304.6 5.6 %copy-start.80 = (f32[8,6,12]{2,1,0:T(8,128)S(1)}, f32[8,6,12]{2,1,0:T(8,128)}, u32[]{:S(2)}) copy-start(f32[8,6,12]{2,1,0:T(8,128)} %copy-done.79) | copy-start | bytes 6916
  304.7 93.5 %all-to-all-start.1 = ((bf16[32,2,256,128]{3,2,1,0:T(8,128)(2,1)}), bf16[32,2,256,128]{3,2,1,0:T(8,128)(2,1)}, u32[]{:S(2)}, u32[]{:S(2)}) async-start(bf16[32,2,256,128]{3,2,1,0:T(8,128)(2,1)} %broadcast_in_dim.136), calls=%async_computation.1 | async-start | bytes 8388608 | tf_op jit(solution)/shard_map/all_to_all | solution.py:394
  311.0 7.2 %collective-permute-start.8 = (bf16[8,6,12,192]{3,2,1,0:T(8,128)(2,1)S(1)}, bf16[8,6,12,192]{3,2,1,0:T(8,128)(2,1)S(1)}, u32[]{:S(2)}, u32[]{:S(2)}) collective-permute-start(bf16[8,6,12,192]{3,2,1,0:T(8,128)(2,1)S(1)} %add_convert_fusion), channel_id=1, source_target_pairs={{64,0},{128,64},{192,128},{65,1},{129,65},{193,129},{66,2},{130,66... | collective-permute-start | bytes 663560 | tf_op jit(solution)/shard_map/ppermute | solution.py:38
  (52 other events, 92.0 us)

commit v2 on v0

v2 whole, which is shorter than its diff:
```python
import functools

import jax
import jax.numpy as jnp
import numpy as np
from jax import lax
from jax.experimental import pallas as pl
from jax.experimental.pallas import tpu as pltpu
from jax.sharding import PartitionSpec as P

MODEL_WIDTH = 192
HEADS = 6
HEAD_SIZE = 32
LEVELS = 8
WIN_LEVELS = 2
WIN_LAT = 6
WIN_LON = 12
BLOCKS = 2
MLP_WIDTH = 768
LAT_DEV = 6
LON_DEV = 12
LEVEL_WINDOWS = 4
WIN_TOKENS = 144
BIAS_SLOTS = 3312

NORM_EPS = 1e-05
MASK_FILL = -10000.0
GELU_C = 0.7978845608028654
GELU_A = 0.044715

TOKENS = LEVELS * LAT_DEV * LON_DEV
QUAD = TOKENS // 4
STACK = HEADS * WIN_TOKENS
GROUPS = WIN_LEVELS * WIN_LAT
OFFSETS = 2 * WIN_LON - 1
PAIR_LANES = GROUPS * OFFSETS
PAIR_PAD = 384
TYPE_ROWS = LEVEL_WINDOWS * HEADS * GROUPS
WEIGHT_ROWS = 3456
TABLE_ROWS = 624
PACK_ROWS = 4096

F32 = jnp.float32
BF16 = jnp.bfloat16


def quad_orders():
    level, row, col = np.meshgrid(
        np.arange(LEVELS), np.arange(LAT_DEV), np.arange(LON_DEV), indexing="ij"
    )
    half_rows, half_cols = WIN_LAT // 2, WIN_LON // 2
    quad = (1 - row // half_rows) * 2 + (1 - col // half_cols)
    place = (quad * LEVELS + level) * (half_rows * half_cols)
    place = place + (row % half_rows) * half_cols + col % half_cols
    split = place.reshape(-1)
    quad_r = (row // half_rows) * 2 + col // half_cols
    from_level = (level + WIN_LEVELS // 2) % LEVELS
    place_r = (quad_r * LEVELS + from_level) * (half_rows * half_cols)
    place_r = place_r + (row % half_rows) * half_cols + col % half_cols
    split_rolled = place_r.reshape(-1)
    join = np.argsort(split)
    join_rolled = np.argsort(split_rolled)
    return [order.astype(np.int32)[None, :] for order in (split, join_rolled, split_rolled, join)]


def dot_nn(a, b):
    return jnp.dot(a, b, preferred_element_type=F32)


def dot_nt(a, b):
    return lax.dot_general(a, b, (((1,), (1,)), ((), ())), preferred_element_type=F32)


def dot_tn(a, b):
    return lax.dot_general(a, b, (((0,), (0,)), ((), ())), preferred_element_type=F32)


def reorder(values, order_row):
    rows = lax.broadcasted_iota(jnp.int32, (TOKENS, TOKENS), 0)
    pick = jnp.where(rows == order_row, 1.0, 0.0).astype(BF16)
    return dot_nn(pick, values).astype(BF16)


def norm_stats(values):
    centred = values - jnp.mean(values, axis=-1, keepdims=True)
    spread = jnp.mean(centred * centred, axis=-1, keepdims=True)
    inv = lax.rsqrt(spread + NORM_EPS)
    return centred * inv, inv


def norm_grad(grad, unit, inv, gain_row):
    gain_grad = jnp.sum(grad * unit, axis=0, keepdims=True)
    grad_unit = grad * gain_row
    first = jnp.mean(grad_unit, axis=-1, keepdims=True)
    second = jnp.mean(grad_unit * unit, axis=-1, keepdims=True)
    return inv * (grad_unit - first - unit * second), gain_grad


def head_masks():
    lane = lax.broadcasted_iota(jnp.int32, (1, MODEL_WIDTH), 1)
    return [
        jnp.logical_and(lane >= h * HEAD_SIZE, lane < (h + 1) * HEAD_SIZE) for h in range(HEADS)
    ]


def stack_heads(values, masks):
    wide = values.astype(F32)
    return jnp.concatenate([jnp.where(m, wide, 0.0) for m in masks], axis=0).astype(BF16)


def fold_heads(stacked, masks):
    total = jnp.where(masks[0], stacked[:WIN_TOKENS], 0.0)
    for h in range(1, HEADS):
        total = jnp.where(masks[h], stacked[h * WIN_TOKENS : (h + 1) * WIN_TOKENS], total)
    return total


def pair_pick(query_col):
    key = lax.broadcasted_iota(jnp.int32, (256, PAIR_PAD), 0)
    lane = lax.broadcasted_iota(jnp.int32, (256, PAIR_PAD), 1)
    group = lax.shift_right_logical(key * 5462, 16)
    key_col = key - group * WIN_LON
    target = group * OFFSETS + (WIN_LON - 1 + query_col) - key_col
    hit = jnp.logical_and(lane == target, key < WIN_TOKENS)
    return jnp.where(hit, 1.0, 0.0).astype(BF16)


def build_bias(table, bias_a, bias_b):
    high = table.astype(BF16)
    rest = table - high.astype(F32)
    middle = rest.astype(BF16)
    low = (rest - middle.astype(F32)).astype(BF16)
    for query_col in range(WIN_LON):
        pick = pair_pick(query_col)
        spread = dot_nt(high, pick) + dot_nt(middle, pick) + dot_nt(low, pick)
        bias_a[pl.ds(query_col, TYPE_ROWS, stride=WIN_LON), :] = spread[:, :128]
        bias_b[pl.ds(query_col, TYPE_ROWS, stride=WIN_LON), :] = spread[:, 128:]


def fold_table(score_a, score_b):
    total = jnp.zeros((TYPE_ROWS, PAIR_PAD), F32)
    for query_col in range(WIN_LON):
        pick = pair_pick(query_col)
        left = score_a[pl.ds(query_col, TYPE_ROWS, stride=WIN_LON), :]
        right = score_b[pl.ds(query_col, TYPE_ROWS, stride=WIN_LON), :]
        total = total + dot_nn(left.astype(BF16), pick[:128])
        total = total + dot_nn(right.astype(BF16), pick[128:])
    return total


def shift_mask(window, lat_row):
    shape = (WIN_TOKENS, WIN_TOKENS)
    half = WIN_TOKENS // 2
    parts = []
    for axis in (0, 1):
        token = lax.broadcasted_iota(jnp.int32, shape, axis)
        upper = token >= half
        inner = jnp.where(upper, token - half, token)
        parts.append((upper, inner >= half // 2))
    rows_differ = jnp.where(parts[0][1] != parts[1][1], 1.0, 0.0) * lat_row
    if window == LEVEL_WINDOWS - 1:
        levels_differ = jnp.where(parts[0][0] != parts[1][0], 1.0, 0.0)
        rows_differ = jnp.maximum(rows_differ, levels_differ)
    return rows_differ * MASK_FILL


def attention_front(unit, gain_row, input_weight, bias_a, bias_b, lat_row, q_ref, k_ref, v_ref, w_ref, mix_ref):
    normed = (unit * gain_row).astype(BF16)
    q_ref[...] = (dot_nn(normed, input_weight[:, :MODEL_WIDTH]) * HEAD_SIZE ** (-0.5)).astype(BF16)
    k_ref[...] = dot_nn(normed, input_weight[:, MODEL_WIDTH : 2 * MODEL_WIDTH]).astype(BF16)
    v_ref[...] = dot_nn(normed, input_weight[:, 2 * MODEL_WIDTH :]).astype(BF16)
    masks = head_masks()
    for window in range(LEVEL_WINDOWS):
        rows = pl.ds(window * WIN_TOKENS, WIN_TOKENS)
        stack_rows = pl.ds(window * STACK, STACK)
        queries = stack_heads(q_ref[rows, :], masks)
        scores = dot_nt(queries, k_ref[rows, :])
        bias = jnp.concatenate(
            [bias_a[stack_rows, :], bias_b[stack_rows, :][:, : WIN_TOKENS - 128]], axis=1
        )
        scores = scores + bias
        if lat_row is not None:
            mask = shift_mask(window, lat_row)
            scores = scores + jnp.concatenate([mask] * HEADS, axis=0)
        scores = jnp.exp(scores - jnp.max(scores, axis=-1, keepdims=True))
        weights = (scores / jnp.sum(scores, axis=-1, keepdims=True)).astype(BF16)
        w_ref[stack_rows, :] = weights
        mixed = dot_nn(weights, v_ref[rows, :])
        mix_ref[rows, :] = fold_heads(mixed, masks).astype(BF16)
    return normed


def gelu_parts(pre):
    square = pre * pre
    tanh = jnp.tanh(GELU_C * (pre + GELU_A * pre * square))
    half = 0.5 * (1.0 + tanh)
    slope = half + 0.5 * pre * (1.0 - tanh * tanh) * (GELU_C * (1.0 + 3.0 * GELU_A * square))
    return pre * half, slope


def pack_columns(out_ref, first, values):
    rows, lanes = values.shape
    for block in range(lanes // 128):
        out_ref[pl.ds(first + block * rows, rows), :] = values[:, block * 128 : (block + 1) * 128].astype(BF16)


def backward(e, x_unit, x_inv, gains, middle, weights4, saved, scores_ab, pack_ref, gproj_ref):
    input_weight, output_weight, expand_weight, reduce_weight = weights4
    q_ref, k_ref, v_ref, w_ref, mix_ref = saved
    score_a, score_b = scores_ab
    masks = head_masks()
    mid_unit, mid_inv = norm_stats(middle.astype(F32))
    gain_mid = gains[1:2, :]
    normed_mid = (mid_unit * gain_mid).astype(BF16)
    hidden, slope = gelu_parts(dot_nn(normed_mid, expand_weight))
    hidden = hidden.astype(BF16)
    grad_pre = (slope * dot_nt(e, reduce_weight)).astype(BF16)
    reduce_grad = dot_tn(hidden, e)
    half_mlp = MLP_WIDTH // 2
    pack_columns(
        pack_ref, 2304, jnp.concatenate([reduce_grad[:half_mlp], reduce_grad[half_mlp:]], axis=1)
    )
    pack_columns(pack_ref, 1152, dot_tn(normed_mid, grad_pre))
    grad_norm, gain_mid_grad = norm_grad(dot_nt(grad_pre, expand_weight), mid_unit, mid_inv, gain_mid)
    grad_middle = e.astype(F32) + grad_norm
    grad_attended = grad_middle.astype(BF16)
    output_grad = dot_tn(mix_ref[...], grad_attended)
    grad_mixture = dot_nt(grad_attended, output_weight).astype(BF16)
    for window in range(LEVEL_WINDOWS):
        base = window * WIN_TOKENS
        rows = pl.ds(base, WIN_TOKENS)
        stack_rows = pl.ds(window * STACK, STACK)
        queries = stack_heads(q_ref[rows, :], masks)
        grads = stack_heads(grad_mixture[base : base + WIN_TOKENS], masks)
        weights = w_ref[stack_rows, :]
        keys = k_ref[rows, :]
        gproj_ref[2, rows, :] = dot_tn(weights, grads).astype(BF16)
        grad_weights = dot_nt(grads, v_ref[rows, :])
        attention = weights.astype(F32)
        moved = attention * grad_weights
        grad_scores = attention * (grad_weights - jnp.sum(moved, axis=-1, keepdims=True))
        score_a[stack_rows, :] = grad_scores[:, :128]
        score_b[stack_rows, :] = jnp.concatenate(
            [grad_scores[:, 128:], jnp.zeros((STACK, 256 - WIN_TOKENS), F32)], axis=1
        )
        score_part = grad_scores.astype(BF16)
        grad_queries = fold_heads(dot_nn(score_part, keys), masks) * HEAD_SIZE ** (-0.5)
        gproj_ref[0, rows, :] = grad_queries.astype(BF16)
        gproj_ref[1, rows, :] = dot_tn(score_part, queries).astype(BF16)
    normed = (x_unit * gains[0:1, :]).astype(BF16)
    parts = [gproj_ref[part] for part in range(3)]
    weight_grads = [dot_tn(normed, part) for part in parts] + [output_grad]
    pack_columns(pack_ref, 0, jnp.concatenate(weight_grads, axis=1))
    grad_normed = dot_nt(parts[0], input_weight[:, :MODEL_WIDTH])
    grad_normed = grad_normed + dot_nt(parts[1], input_weight[:, MODEL_WIDTH : 2 * MODEL_WIDTH])
    grad_normed = grad_normed + dot_nt(parts[2], input_weight[:, 2 * MODEL_WIDTH :])
    grad_normed = grad_normed.astype(BF16).astype(F32)
    grad_in, gain_in_grad = norm_grad(grad_normed, x_unit, x_inv, gains[0:1, :])
    folded = fold_table(score_a, score_b)
    pack_columns(pack_ref, WEIGHT_ROWS, folded[:, :256])
    rest_rows = []
    for window in range(LEVEL_WINDOWS):
        pieces = [
            folded[(window * HEADS + h) * GROUPS : (window * HEADS + h + 1) * GROUPS, 256:PAIR_LANES]
            for h in range(HEADS)
        ]
        pieces.append(jnp.zeros((GROUPS, 128 - HEADS * (PAIR_LANES - 256)), F32))
        rest_rows.append(jnp.concatenate(pieces, axis=1))
    gain_flat = jnp.concatenate([gain_in_grad, gain_mid_grad], axis=1)
    gain_rows = [gain_flat[:, i * 128 : (i + 1) * 128] for i in range(3)]
    tail = rest_rows + gain_rows + [jnp.zeros((13, 128), F32)]
    pack_ref[pl.ds(WEIGHT_ROWS + 2 * TYPE_ROWS, 64), :] = jnp.concatenate(tail, axis=0).astype(BF16)
    return (grad_middle + grad_in).astype(BF16)


def forward_kernel(
    x_ref, gains_ref, wi_ref, wo_ref, we_ref, wr_ref, table_ref, order_ref,
    quad0, quad1, quad2, quad3, q_ref, k_ref, v_ref, w_ref, mix_ref, mid_ref,
    bias_a, bias_b,
):
    build_bias(table_ref[...], bias_a, bias_b)
    gains = gains_ref[...]
    values = x_ref[...].astype(F32)
    unit, _ = norm_stats(values)
    attention_front(
        unit, gains[0:1, :], wi_ref[...], bias_a, bias_b, None, q_ref, k_ref, v_ref, w_ref, mix_ref
    )
    middle = (values + dot_nn(mix_ref[...], wo_ref[...])).astype(BF16)
    mid_ref[...] = middle
    mid_f = middle.astype(F32)
    mid_unit, _ = norm_stats(mid_f)
    normed_mid = (mid_unit * gains[1:2, :]).astype(BF16)
    hidden, _ = gelu_parts(dot_nn(normed_mid, we_ref[...]))
    output = (mid_f + dot_nn(hidden.astype(BF16), wr_ref[...])).astype(BF16)
    quads = reorder(output, order_ref[...])
    for index, quad in enumerate((quad0, quad1, quad2, quad3)):
        quad[...] = quads[index * QUAD : (index + 1) * QUAD]


def turn_kernel(
    x0, x1, x2, x3, e0, e1, e2, e3, lat_ref, gains_ref, wi_ref, wo_ref, we_ref, wr_ref, table_ref,
    join_ref, split_ref, quad0, quad1, quad2, quad3, pack_ref,
    bias_a, bias_b, q_ref, k_ref, v_ref, w_ref, mix_ref, gproj_ref,
):
    build_bias(table_ref[...], bias_a, bias_b)
    gains = gains_ref[...]
    join = join_ref[...]
    block_in = reorder(jnp.concatenate([x0[...], x1[...], x2[...], x3[...]], axis=0), join)
    e = reorder(jnp.concatenate([e0[...], e1[...], e2[...], e3[...]], axis=0), join)
    values = block_in.astype(F32)
    unit, inv = norm_stats(values)
    input_weight, output_weight = wi_ref[...], wo_ref[...]
    attention_front(
        unit, gains[0:1, :], input_weight, bias_a, bias_b, lat_ref[0:1, 0:1], q_ref, k_ref, v_ref,
        w_ref, mix_ref,
    )
    attended = dot_nn(mix_ref[...], output_weight).astype(BF16).astype(F32)
    middle = (values + attended).astype(BF16)
    result = backward(
        e, unit, inv, gains, middle, (input_weight, output_weight, we_ref[...], wr_ref[...]),
        (q_ref, k_ref, v_ref, w_ref, mix_ref), (bias_a, bias_b), pack_ref, gproj_ref,
    )
    quads = reorder(result, split_ref[...])
    for index, quad in enumerate((quad0, quad1, quad2, quad3)):
        quad[...] = quads[index * QUAD : (index + 1) * QUAD]


def backward_kernel(
    x_ref, e0, e1, e2, e3, gains_ref, wi_ref, wo_ref, we_ref, wr_ref, join_ref,
    q_ref, k_ref, v_ref, w_ref, mix_ref, mid_ref, out_ref, pack_ref, score_a, score_b, gproj_ref,
):
    e = reorder(jnp.concatenate([e0[...], e1[...], e2[...], e3[...]], axis=0), join_ref[...])
    unit, inv = norm_stats(x_ref[...].astype(F32))
    out_ref[...] = backward(
        e, unit, inv, gains_ref[...], mid_ref[...],
        (wi_ref[...], wo_ref[...], we_ref[...], wr_ref[...]),
        (q_ref, k_ref, v_ref, w_ref, mix_ref), (score_a, score_b), pack_ref, gproj_ref,
    )


LIMIT = 60 * 1024 * 1024
TOKEN_SHAPE = jax.ShapeDtypeStruct((TOKENS, MODEL_WIDTH), BF16)
QUAD_SHAPE = jax.ShapeDtypeStruct((QUAD, MODEL_WIDTH), BF16)
WEIGHT_SHAPE = jax.ShapeDtypeStruct((LEVEL_WINDOWS * STACK, WIN_TOKENS), BF16)
PACK_SHAPE = jax.ShapeDtypeStruct((PACK_ROWS, 128), BF16)


def tall_scratch():
    return pltpu.VMEM((LEVEL_WINDOWS * STACK, 128), F32)


def token_scratch():
    return pltpu.VMEM((TOKENS, MODEL_WIDTH), BF16)


def call(kernel, outs, scratch, *args):
    return pl.pallas_call(
        kernel,
        out_shape=outs,
        scratch_shapes=scratch,
        compiler_params=pltpu.CompilerParams(vmem_limit_bytes=LIMIT),
    )(*args)


def exchange(quads, by):
    ring, sides = lax.axis_size("lon"), lax.axis_size("lat")
    lon_pairs = [(i, (i + by) % ring) for i in range(ring)]
    swap = [(i, i ^ 1) for i in range(sides)]
    both = [
        (i * sides + j, ((i + by) % ring) * sides + (j ^ 1)) for i in range(ring) for j in range(sides)
    ]
    return (
        quads[0],
        lax.ppermute(quads[1], "lon", lon_pairs),
        lax.ppermute(quads[2], "lat", swap),
        lax.ppermute(quads[3], ("lon", "lat"), both),
    )


def pair_rows(tables):
    shaped = tables.reshape(
        BLOCKS, LEVEL_WINDOWS, HEADS, WIN_LEVELS, WIN_LEVELS, WIN_LAT, WIN_LAT * OFFSETS
    )
    shaped = shaped.swapaxes(4, 5).reshape(BLOCKS, TYPE_ROWS, PAIR_LANES)
    return jnp.pad(shaped, ((0, 0), (0, 0), (0, PAIR_PAD - PAIR_LANES)))


def reduce_packs(pack):
    ring = lax.axis_size("lon")
    spread = lax.all_to_all(
        pack.reshape(ring, PACK_ROWS // ring, 128), "lon", split_axis=0, concat_axis=0, tiled=True
    )
    mine = jnp.sum(spread.astype(F32), axis=0).astype(BF16)
    other = lax.ppermute(mine, "lat", [(0, 1), (1, 0)])
    first = lax.axis_index("lat") == 0
    pair = jnp.stack([jnp.where(first, mine, other), jnp.where(first, other, mine)])
    pair = jnp.broadcast_to(pair[None], (ring,) + pair.shape)
    whole = lax.all_to_all(pair, "lon", split_axis=0, concat_axis=0, tiled=True)
    return whole.swapaxes(0, 1).reshape(2, PACK_ROWS, 128).astype(F32)


def columns(values, first, rows, blocks):
    part = values[first : first + rows * blocks].reshape(blocks, rows, 128)
    return part.swapaxes(0, 1).reshape(rows, blocks * 128)


def unpack(halves):
    both = halves[0, :WEIGHT_ROWS] + halves[1, :WEIGHT_ROWS]
    front = columns(both, 0, MODEL_WIDTH, 6)
    expand = columns(both, 1152, MODEL_WIDTH, 6)
    tall = columns(both, 2304, MLP_WIDTH // 2, 3)
    reduce = jnp.concatenate([tall[:, :MODEL_WIDTH], tall[:, MODEL_WIDTH:]], axis=0)
    tables = []
    for side in range(2):
        wide = columns(halves[side], WEIGHT_ROWS, TYPE_ROWS, 2)
        rest = halves[side, WEIGHT_ROWS + 2 * TYPE_ROWS : WEIGHT_ROWS + TABLE_ROWS]
        rest = rest[:, :120].reshape(LEVEL_WINDOWS, GROUPS, HEADS, 20).swapaxes(1, 2)
        full = jnp.concatenate([wide, rest.reshape(TYPE_ROWS, 20)], axis=1)
        full = full.reshape(
            LEVEL_WINDOWS, HEADS, WIN_LEVELS, WIN_LAT, WIN_LEVELS, WIN_LAT * OFFSETS
        )
        tables.append(full.swapaxes(3, 4).reshape(LEVEL_WINDOWS, HEADS, BIAS_SLOTS))
    table = jnp.stack(tables, axis=1)
    gain = halves[0] + halves[1]
    gain = gain[WEIGHT_ROWS + TABLE_ROWS : WEIGHT_ROWS + TABLE_ROWS + 3].reshape(2, MODEL_WIDTH)
    return front[:, : 3 * MODEL_WIDTH], front[:, 3 * MODEL_WIDTH :], expand, reduce, gain, table


def on_device(
    inputs, grad_output, norm_gains, input_weight, output_weight, expand_weight, reduce_weight,
    bias_table,
):
    lat_index = lax.axis_index("lat")
    orders = [jnp.asarray(order) for order in quad_orders()]
    split, join_rolled, split_rolled, join = orders
    tables = pair_rows(
        lax.dynamic_index_in_dim(bias_table[0], lat_index, axis=2, keepdims=False)
    )
    weights = [
        (norm_gains[0, b], input_weight[0, b], output_weight[0, b], expand_weight[0, b], reduce_weight[0, b])
        for b in range(BLOCKS)
    ]
    tokens = inputs[0].reshape(TOKENS, MODEL_WIDTH)
    grads = grad_output[0].reshape(TOKENS, MODEL_WIDTH)

    def split_kernel(x_ref, order_ref, *quads):
        parts = reorder(x_ref[...], order_ref[...])
        for index, quad in enumerate(quads):
            quad[...] = parts[index * QUAD : (index + 1) * QUAD]

    grad_quads = exchange(call(split_kernel, (QUAD_SHAPE,) * 4, [], grads, split), -1)
    outs = call(
        forward_kernel,
        (QUAD_SHAPE,) * 4 + (TOKEN_SHAPE,) * 3 + (WEIGHT_SHAPE,) + (TOKEN_SHAPE,) * 2,
        [tall_scratch(), tall_scratch()],
        tokens, *weights[0], tables[0], split,
    )
    saved = outs[4:]
    block_quads = exchange(outs[:4], -1)
    lat_row = jnp.full((8, 128), lat_index, F32)
    outs = call(
        turn_kernel,
        (QUAD_SHAPE,) * 4 + (PACK_SHAPE,),
        [tall_scratch(), tall_scratch()] + [token_scratch() for _ in range(3)]
        + [pltpu.VMEM(WEIGHT_SHAPE.shape, BF16), token_scratch(),
           pltpu.VMEM((3, TOKENS, MODEL_WIDTH), BF16)],
        *block_quads, *grad_quads, lat_row, *weights[1], tables[1], join_rolled, split_rolled,
    )
    pack_late = outs[4]
    flow_quads = exchange(outs[:4], 1)
    grad_flow, pack_early = call(
        backward_kernel,
        (TOKEN_SHAPE, PACK_SHAPE),
        [tall_scratch(), tall_scratch(), pltpu.VMEM((3, TOKENS, MODEL_WIDTH), BF16)],
        tokens, *flow_quads, *weights[0], join, *saved,
    )
    upstream = lax.ppermute(
        grad_flow, "section", [(i, i - 1) for i in range(1, lax.axis_size("section"))]
    )
    upstream = upstream.reshape(1, LEVELS, LAT_DEV, LON_DEV, MODEL_WIDTH)
    lat_total = LAT_DEV * lax.axis_size("lat")
    grad_scale = float(LEVELS * lat_total * LON_DEV * lax.axis_size("lon")) ** (-0.5)
    results = [unpack(reduce_packs(pack)) for pack in (pack_early, pack_late)]
    stacked = [jnp.stack([results[b][index] for b in range(BLOCKS)])[None] for index in range(6)]
    return (upstream,) + tuple(total * grad_scale for total in stacked[:5]) + (stacked[5],)


def solution(mesh):
    return jax.shard_map(
        on_device,
        mesh=mesh,
        in_specs=(
            P("section", None, "lat", "lon", None),
            P("section", None, "lat", "lon", None),
            P("section", None, None, None),
            P("section", None, None, None),
            P("section", None, None, None),
            P("section", None, None, None),
            P("section", None, None, None),
            P("section", None, None, None, None, None),
        ),
        out_specs=(
            P("section", None, "lat", "lon", None),
            P("section", None, None, None),
            P("section", None, None, None),
            P("section", None, None, None),
            P("section", None, None, None),
            P("section", None, None, None),
            P("section", None, None, None, None, None),
        ),
        check_vma=False,
    )
```

time: 974 us -> 279 us (0.29)
  waiting for transfers between devices: 556 us -> 114 us
  blocking collectives: 178 us -> 0 us
  matrix products: 77.8 us -> 0 us
  Pallas kernels: 0 us -> 41.7 us
  starting transfers between devices: 16.9 us -> 52 us
  other arithmetic: 43.3 us -> 14.6 us
  local copies, waits for them, and re-layouts: 78.4 us -> 51.8 us
  between operations: 16.2 us -> 1.54 us
    psum x1 -> x0, waiting for transfers between devices: 523 us -> none  [on_device(): lax.psum((stacked[0], stacked[1], stacked[2], stacked[3], stacked[4], ful...]
    psum x1 -> x0, blocking collectives: 178 us -> none  [on_device(): lax.psum((stacked[0], stacked[1], stacked[2], stacked[3], stacked[4], ful...]
    dot_general x39 -> x0, matrix products: 77.8 us -> none  [the longest x2 11.9 us: table_grad(): jnp.einsum('...rm,gm->...rg', shaped, spread_map, precision=lax.Precision...]
    all_to_all x0 -> x4, waiting for transfers between devices: none -> 76.3 us  [the longest x2 55.8 us: reduce_packs(): whole = lax.all_to_all(pair, 'lon', split_axis=0, concat_axis=0, tiled=True)]
    pallas_call x0 -> x4, Pallas kernels: none -> 41.7 us  [call(): pl.pallas_call(kernel, out_shape=outs, scratch_shapes=scratch, compiler_p...]
    all_to_all x0 -> x4, starting transfers between devices: none -> 22.6 us  [the longest x2 11.5 us: reduce_packs(): whole = lax.all_to_all(pair, 'lon', split_axis=0, concat_axis=0, tiled=True)]
    ppermute x9 -> x12, starting transfers between devices: 16.9 us -> 29.4 us  [the longest x3 10.5 us: exchange(): lax.ppermute(quads[1], 'lon', lon_pairs)]
    another operation x18 -> x12, local copies, waits for them, and re-layouts: 21.1 us -> 9.52 us  [the longest x4 4.77 us: unpack(): table = jnp.stack(tables, axis=1)]
  transfers between devices with their start and end apart: 10 -> 16, of which waited for: 7 -> 10; matrix products, arithmetic and copies ran while one was open for 3% -> 14% of each run, Pallas kernels for 0% -> 8%
where the time goes in v2:
time: 279 us; the launch traced here: 276 us
  waiting for transfers between devices  114 us (41%)
  starting transfers between devices  52 us (19%)
  local copies, waits for them, and re-layouts  51.8 us (19%)
  Pallas kernels  41.7 us (15%)
  other arithmetic  14.6 us (5%)
    all_to_all x2, waiting for transfers between devices, reduce_packs(): whole = lax.all_to_all(pair, 'lon', split_axis=0, concat_axis=0, tiled=True)  55.8 us
    pallas_call x4, Pallas kernels, call(): pl.pallas_call(kernel, out_shape=outs, scratch_shapes=scratch, compiler_p...  41.7 us
    ppermute x3, waiting for transfers between devices, exchange(): lax.ppermute(quads[1], 'lon', lon_pairs)  20.8 us
    all_to_all x2, waiting for transfers between devices, reduce_packs(): lax.all_to_all(pack.reshape(ring, PACK_ROWS // ring, 128), 'lon', split_a...  20.5 us
    all_to_all x2, starting transfers between devices, reduce_packs(): whole = lax.all_to_all(pair, 'lon', split_axis=0, concat_axis=0, tiled=True)  11.5 us
    all_to_all x2, starting transfers between devices, reduce_packs(): lax.all_to_all(pack.reshape(ring, PACK_ROWS // ring, 128), 'lon', split_a...  11.1 us
    ppermute x3, starting transfers between devices, exchange(): lax.ppermute(quads[1], 'lon', lon_pairs)  10.5 us
    unnamed x72, local copies, waits for them, and re-layouts  6.57 us
  transfers between devices with their start and end apart: 16, of which 10 were waited for; matrix products, arithmetic and copies ran while one was open for 14% of the time, Pallas kernels for 8%

profile of v2, /device:TPU:8, one launch (start us, length us, event | category | flops | bytes accessed | tf_op | source)
XLA Modules:
  0.0 275.8 jit_solution(4552542028322867579)
XLA Ops:
  0.7 1.2 copy.78
  2.7 2.0 shard_map.172
  4.7 8.1 %collective-permute-start.3 = (bf16[144,192]{1,0:T(8,128)(2,1)}, bf16[144,192]{1,0:T(8,128)(2,1)}, u32[]{:S(2)}, u32[]{:S(2)}) collective-permute-start(bf16[144,192]{1,0:T(8,128)(2,1)} %get-tuple-element.33), channel_id=1, source_target_pairs={{0,62},{2,0},{4,2},{6,4},{8,6},{10,8},{12,10},{14,12},{16,14},{18,... | collective-permute-start | bytes 165896 | tf_op jit(solution)/shard_map/ppermute | solution.py:374
  12.8 2.3 collective-permute-start.4
  15.1 1.7 collective-permute-start.5
  16.7 1.3 slice_bitcast_fusion.14
  21.3 1.5 reshape.322
  23.5 1.0 reshape.323
  24.5 1.0 fusion.1
  26.4 0.9 copy.102
  27.3 9.0 %shard_map.171 = (bf16[144,192]{1,0:T(8,128)(2,1)}, bf16[144,192]{1,0:T(8,128)(2,1)}, bf16[144,192]{1,0:T(8,128)(2,1)}, bf16[144,192]{1,0:T(8,128)(2,1)}, bf16[5...) custom-call(bf16[576,192]{1,0:T(8,128)(2,1)} %reshape_squeeze.6.x_re, ...), custom_call_target="tpu_custom_call" | custom-call | tf_op jit(solution)/shard_map/pallas_call | solution.py:357
  36.9 2.3 collective-permute-start.1
  39.2 1.6 collective-permute-start.2
  40.8 0.9 copy.103
  41.7 1.2 collective-permute-done.1.x2
  43.0 3.6 %collective-permute-done.2.x3 = bf16[144,192]{1,0:T(8,128)(2,1)S(1)} collective-permute-done((bf16[144,192]{1,0:T(8,128)(2,1)}, bf16[144,192]{1,0:T(8,128)(2,1)S(1)}, u32[]{:S(2)}, u32[]{:S(2)}) %collective-permute-start.2) | collective-permute-done | bytes 55328 | tf_op jit(solution)/shard_map/ppermute | solution.py:376
  47.2 17.8 %shard_map.173 = (bf16[144,192]{1,0:T(8,128)(2,1)}, bf16[144,192]{1,0:T(8,128)(2,1)}, bf16[144,192]{1,0:T(8,128)(2,1)}, bf16[144,192]{1,0:T(8,128)(2,1)}, bf16[4096,128]{1,0:T(8,128)(2,1)}) custom-call(bf16[144,192]{1,0:T(8,128)(2,1)} %get-tuple-element.28.x0, bf16[144,192]{1,0:T(8,128)(2,1)} %copy-done.21, bf16[144,192]{1,0:T(8,128)(2,1)} %copy-done.22, ...), custom_call_target="tpu_custom_call" | custom-call | tf_op jit(solution)/shard_map/pallas_call | solution.py:357
  65.1 5.9 %all-to-all-start.2 = ((bf16[32,128,128]{2,1,0:T(8,128)(2,1)}), bf16[32,128,128]{2,1,0:T(8,128)(2,1)S(1)}, u32[]{:S(2)}, u32[]{:S(2)}) async-start(bf16[32,128,128]{2,1,0:T(8,128)(2,1)} %bitcast.181), calls=%async_computation.2 | async-start | bytes 2097152 | tf_op jit(solution)/shard_map/all_to_all | solution.py:390
  71.0 1.9 collective-permute-start.6
  72.8 1.2 collective-permute-start.7
  74.1 3.2 %collective-permute-start.8 = (bf16[144,192]{1,0:T(8,128)(2,1)S(1)}, bf16[144,192]{1,0:T(8,128)(2,1)S(1)}, u32[]{:S(2)}, u32[]{:S(2)}) collective-permute-start(bf16[144,192]{1,0:T(8,128)(2,1)S(1)} %copy-done.28), channel_id=1, source_target_pairs={{0,3},{1,2},{2,5},{3,4},{4,7},{5,6},{6,9},{7,8},{8,11},{9,10},{10,... | collective-permute-start | bytes 165896 | tf_op jit(solution)/shard_map/ppermute | solution.py:376
  77.3 20.8 %collective-permute-done.6.e1 = bf16[144,192]{1,0:T(8,128)(2,1)S(1)} collective-permute-done((bf16[144,192]{1,0:T(8,128)(2,1)S(1)}, bf16[144,192]{1,0:T(8,128)(2,1)S(1)}, u32[]{:S(2)}, u32[]{:S(2)}) %collective-permute-start.6) | collective-permute-done | bytes 55328 | tf_op jit(solution)/shard_map/ppermute | solution.py:374
  98.0 1.8 collective-permute-done.8.e3
  100.5 12.9 %shard_map.174 = (bf16[576,192]{1,0:T(8,128)(2,1)}, bf16[4096,128]{1,0:T(8,128)(2,1)}) custom-call(bf16[576,192]{1,0:T(8,128)(2,1)} %reshape_squeeze.6.x_ref, bf16[144,192]{1,0:T(8,128)(2,1)} %get-tuple-element.36.e0, bf16[144,192]{1,0:T(8,128)(2,1)} %copy-done.24, bf16[144,192]{1,0:T(8,128)(2,1)} %copy-done.25, bf16[144,192]{1,0:T(8,128)(2,1)} %copy-done.26, ...), custom_call_target="tpu_custom_call" | custom-call | tf_op jit(solution)/shard_map/pallas_call | solution.py:357
  113.4 5.2 %all-to-all-start = ((bf16[32,128,128]{2,1,0:T(8,128)(2,1)}), bf16[32,128,128]{2,1,0:T(8,128)(2,1)S(1)}, u32[]{:S(2)}, u32[]{:S(2)}) async-start(bf16[32,128,128]{2,1,0:T(8,128)(2,1)} %bitcast.182), calls=%async_computation | async-start | bytes 2097152 | tf_op jit(solution)/shard_map/all_to_all | solution.py:390
  118.8 2.3 collective-permute-start.11
  121.1 3.2 %collective-permute-done.11 = bf16[128,128]{1,0:T(8,128)(2,1)S(1)} collective-permute-done((bf16[128,128]{1,0:T(8,128)(2,1)S(1)}, bf16[128,128]{1,0:T(8,128)(2,1)S(1)}, u32[]{:S(2)}, u32[]{:S(2)}) %collective-permute-start.11) | collective-permute-done | bytes 32800 | tf_op jit(solution)/shard_map/ppermute | solution.py:394
  124.3 20.5 %all-to-all-done = bf16[32,128,128]{2,1,0:T(8,128)(2,1)S(1)} async-done(((bf16[32,128,128]{2,1,0:T(8,128)(2,1)}), bf16[32,128,128]{2,1,0:T(8,128)(2,1)S(1)}, u32[]{:S(2)}, u32[]{:S(2)}) %all-to-all-start) | async-done | bytes 1048608 | tf_op jit(solution)/shard_map/all_to_all | solution.py:390
  144.8 1.8 broadcast_in_dim.10
  146.7 5.4 %all-to-all-start.3 = ((bf16[32,2,128,128]{3,2,1,0:T(8,128)(2,1)}), bf16[32,2,128,128]{3,2,1,0:T(8,128)(2,1)S(1)}, u32[]{:S(2)}, u32[]{:S(2)}) async-start(bf16[32,2,128,128]{3,2,1,0:T(8,128)(2,1)} %broadcast_in_dim.10), calls=%async_computation.3 | async-start | bytes 4194304 | tf_op jit(solution)/shard_map/all_to_all | solution.py:398
  152.1 1.4 reduce_sum.24
  153.5 2.2 collective-permute-start.10
  155.7 3.3 %collective-permute-done.10 = bf16[128,128]{1,0:T(8,128)(2,1)S(1)} collective-permute-done((bf16[128,128]{1,0:T(8,128)(2,1)S(1)}, bf16[128,128]{1,0:T(8,128)(2,1)S(1)}, u32[]{:S(2)}, u32[]{:S(2)}) %collective-permute-start.10) | collective-permute-done | bytes 32800 | tf_op jit(solution)/shard_map/ppermute | solution.py:394
  159.0 40.8 %all-to-all-done.3 = bf16[32,2,128,128]{3,2,1,0:T(8,128)(2,1)S(1)} async-done(((bf16[32,2,128,128]{3,2,1,0:T(8,128)(2,1)}), bf16[32,2,128,128]{3,2,1,0:T(8,128)(2,1)S(1)}, u32[]{:S(2)}, u32[]{:S(2)}) %all-to-all-start.3) | async-done | bytes 2097184 | tf_op jit(solution)/shard_map/all_to_all | solution.py:398
  199.8 2.0 broadcast_in_dim.9
  201.8 6.1 %all-to-all-start.1 = ((bf16[32,2,128,128]{3,2,1,0:T(8,128)(2,1)}), bf16[32,2,128,128]{3,2,1,0:T(8,128)(2,1)S(1)}, u32[]{:S(2)}, u32[]{:S(2)}) async-start(bf16[32,2,128,128]{3,2,1,0:T(8,128)(2,1)} %broadcast_in_dim.9), calls=%async_computation.1 | async-start | bytes 4194304 | tf_op jit(solution)/shard_map/all_to_all | solution.py:398
  207.9 2.1 collective-permute-start.9
  210.0 4.0 %collective-permute-done.9 = bf16[576,192]{1,0:T(8,128)(2,1)S(1)} collective-permute-done((bf16[576,192]{1,0:T(8,128)(2,1)S(1)}, bf16[576,192]{1,0:T(8,128)(2,1)S(1)}, u32[]{:S(2)}, u32[]{:S(2)}) %collective-permute-start.9) | collective-permute-done | bytes 221216 | tf_op jit(solution)/shard_map/ppermute | solution.py:477
  215.0 2.1 convert_bitcast_fusion
  217.1 2.3 copy.82
  221.5 1.1 fusion.3
  223.1 2.2 slice_add_fusion.2
  225.3 1.1 fusion.5
  226.4 1.0 copy.87
  227.5 1.3 reshape.356
  228.8 1.3 reshape.351
  230.2 1.2 copy.96
  231.4 1.2 stack_reshape.18
  232.6 1.2 copy.99
  233.7 1.2 stack_reshape.19
  234.9 1.4 copy.85
  236.4 1.0 stack.87
  237.3 1.1 copy.116
  238.4 1.9 fusion.7
  240.3 15.0 %all-to-all-done.1 = bf16[32,2,128,128]{3,2,1,0:T(8,128)(2,1)S(1)} async-done(((bf16[32,2,128,128]{3,2,1,0:T(8,128)(2,1)}), bf16[32,2,128,128]{3,2,1,0:T(8,128)(2,1)S(1)}, u32[]{:S(2)}, u32[]{:S(2)}) %all-to-all-start.1) | async-done | bytes 2097184 | tf_op jit(solution)/shard_map/all_to_all | solution.py:398
  257.1 0.9 slice_bitcast_fusion.6
  262.7 0.9 pad_maximum_fusion
  264.3 1.2 stack_reshape.16
  265.7 1.2 stack_reshape.17
  267.4 1.4 maximum_bitcast_fusion.1
  269.1 1.7 copy.101
  271.5 1.1 maximum_multiply_fusion.1
  272.7 1.1 maximum_multiply_fusion
  273.8 1.0 maximum_multiply_fusion.2
  (137 shorter events, 20.8 us)
Async XLA Ops:
  0.6 19.8 %copy-start = (f32[1,2,4,2,6,3312]{5,3,4,2,1,0:T(2,128)S(1)}, f32[1,2,4,2,6,3312]{5,3,4,2,1,0:T(2,128)}, u32[]{:S(2)}) copy-start(f32[1,2,4,2,6,3312]{5,3,4,2,1,0:T(2,128)} %param.19) | copy-start | bytes 3815428
  0.7 17.4 %copy-start.20 = (bf16[1,2,192,192]{3,2,1,0:T(8,128)(2,1)S(1)}, bf16[1,2,192,192]{3,2,1,0:T(8,128)(2,1)}, u32[]{:S(2)}) copy-start(bf16[1,2,192,192]{3,2,1,0:T(8,128)(2,1)} %param.16) | copy-start | bytes 442372
  0.7 18.1 %copy-start.18 = (bf16[1,2,192,576]{3,2,1,0:T(8,128)(2,1)S(1)}, bf16[1,2,192,576]{3,2,1,0:T(8,128)(2,1)}, u32[]{:S(2)}) copy-start(bf16[1,2,192,576]{3,2,1,0:T(8,128)(2,1)} %param.15) | copy-start | bytes 1327108
  0.7 18.9 %copy-start.14 = (bf16[1,2,192,768]{3,2,1,0:T(8,128)(2,1)S(1)}, bf16[1,2,192,768]{3,2,1,0:T(8,128)(2,1)}, u32[]{:S(2)}) copy-start(bf16[1,2,192,768]{3,2,1,0:T(8,128)(2,1)} %param.17) | copy-start | bytes 1769476
  1.9 18.6 %copy-start.15 = (bf16[1,2,768,192]{2,3,1,0:T(8,128)(2,1)S(1)}, bf16[1,2,768,192]{2,3,1,0:T(8,128)(2,1)}, u32[]{:S(2)}) copy-start(bf16[1,2,768,192]{2,3,1,0:T(8,128)(2,1)} %param.18) | copy-start | bytes 1769476
  4.7 34.5 %collective-permute-start.3 = (bf16[144,192]{1,0:T(8,128)(2,1)}, bf16[144,192]{1,0:T(8,128)(2,1)}, u32[]{:S(2)}, u32[]{:S(2)}) collective-permute-start(bf16[144,192]{1,0:T(8,128)(2,1)} %get-tuple-element.33), channel_id=1, source_target_pairs={{0,62},{2,0},{4,2},{6,4},{8,6},{10,8},{12,10},{14,12},{16,14},{18,... | collective-permute-start | bytes 165896 | tf_op jit(solution)/shard_map/ppermute | solution.py:374
  12.8 28.9 %collective-permute-start.4 = (bf16[144,192]{1,0:T(8,128)(2,1)}, bf16[144,192]{1,0:T(8,128)(2,1)}, u32[]{:S(2)}, u32[]{:S(2)}) collective-permute-start(bf16[144,192]{1,0:T(8,128)(2,1)} %get-tuple-element.34), channel_id=1, source_target_pairs={{0,1},{1,0},{2,3},{3,2},{4,5},{5,4},{6,7},{7,6},{8,9},{9,8},{10,11... | collective-permute-start | bytes 165896 | tf_op jit(solution)/shard_map/ppermute | solution.py:375
  15.1 26.7 %collective-permute-start.5 = (bf16[144,192]{1,0:T(8,128)(2,1)}, bf16[144,192]{1,0:T(8,128)(2,1)}, u32[]{:S(2)}, u32[]{:S(2)}) collective-permute-start(bf16[144,192]{1,0:T(8,128)(2,1)} %get-tuple-element.35), channel_id=1, source_target_pairs={{0,63},{1,62},{2,1},{3,0},{4,3},{5,2},{6,5},{7,4},{8,7},{9,6},{10,... | collective-permute-start | bytes 165896 | tf_op jit(solution)/shard_map/ppermute | solution.py:376
  23.5 2.0 copy-start.19
  36.3 5.4 %collective-permute-start = (bf16[144,192]{1,0:T(8,128)(2,1)}, bf16[144,192]{1,0:T(8,128)(2,1)S(1)}, u32[]{:S(2)}, u32[]{:S(2)}) collective-permute-start(bf16[144,192]{1,0:T(8,128)(2,1)} %get-tuple-element.29), channel_id=1, source_target_pairs={{0,62},{2,0},{4,2},{6,4},{8,6},{10,8},{12,10},{14,12},{16,14},{18,... | collective-permute-start | bytes 165896 | tf_op jit(solution)/shard_map/ppermute | solution.py:374
  36.9 6.1 %collective-permute-start.1 = (bf16[144,192]{1,0:T(8,128)(2,1)}, bf16[144,192]{1,0:T(8,128)(2,1)S(1)}, u32[]{:S(2)}, u32[]{:S(2)}) collective-permute-start(bf16[144,192]{1,0:T(8,128)(2,1)} %get-tuple-element.30), channel_id=1, source_target_pairs={{0,1},{1,0},{2,3},{3,2},{4,5},{5,4},{6,7},{7,6},{8,9},{9,8},{10,11... | collective-permute-start | bytes 165896 | tf_op jit(solution)/shard_map/ppermute | solution.py:375
  39.2 7.4 %collective-permute-start.2 = (bf16[144,192]{1,0:T(8,128)(2,1)}, bf16[144,192]{1,0:T(8,128)(2,1)S(1)}, u32[]{:S(2)}, u32[]{:S(2)}) collective-permute-start(bf16[144,192]{1,0:T(8,128)(2,1)} %get-tuple-element.31), channel_id=1, source_target_pairs={{0,63},{1,62},{2,1},{3,0},{4,3},{5,2},{6,5},{7,4},{8,7},{9,6},{10,... | collective-permute-start | bytes 165896 | tf_op jit(solution)/shard_map/ppermute | solution.py:376
  41.7 5.5 %copy-start.21 = (bf16[144,192]{1,0:T(8,128)(2,1)}, bf16[144,192]{1,0:T(8,128)(2,1)S(1)}, u32[]{:S(2)}) copy-start(bf16[144,192]{1,0:T(8,128)(2,1)S(1)} %collective-permute-done.x1) | copy-start | bytes 165892
  43.0 4.2 %copy-start.22 = (bf16[144,192]{1,0:T(8,128)(2,1)}, bf16[144,192]{1,0:T(8,128)(2,1)S(1)}, u32[]{:S(2)}) copy-start(bf16[144,192]{1,0:T(8,128)(2,1)S(1)} %collective-permute-done.1.x2) | copy-start | bytes 165892
  46.6 0.6 copy-start.23
  65.0 5.9 %copy-start.30 = (bf16[144,192]{1,0:T(8,128)(2,1)S(1)}, bf16[144,192]{1,0:T(8,128)(2,1)}, u32[]{:S(2)}) copy-start(bf16[144,192]{1,0:T(8,128)(2,1)} %get-tuple-element.37) | copy-start | bytes 165892
  65.0 7.8 %copy-start.29 = (bf16[144,192]{1,0:T(8,128)(2,1)S(1)}, bf16[144,192]{1,0:T(8,128)(2,1)}, u32[]{:S(2)}) copy-start(bf16[144,192]{1,0:T(8,128)(2,1)} %get-tuple-element.38) | copy-start | bytes 165892
  65.1 9.0 %copy-start.28 = (bf16[144,192]{1,0:T(8,128)(2,1)S(1)}, bf16[144,192]{1,0:T(8,128)(2,1)}, u32[]{:S(2)}) copy-start(bf16[144,192]{1,0:T(8,128)(2,1)} %get-tuple-element.39) | copy-start | bytes 165892
  65.1 48.3 %all-to-all-start.2 = ((bf16[32,128,128]{2,1,0:T(8,128)(2,1)}), bf16[32,128,128]{2,1,0:T(8,128)(2,1)S(1)}, u32[]{:S(2)}, u32[]{:S(2)}) async-start(bf16[32,128,128]{2,1,0:T(8,128)(2,1)} %bitcast.181), calls=%async_computation.2 | async-start | bytes 2097152 | tf_op jit(solution)/shard_map/all_to_all | solution.py:390
  71.0 27.1 %collective-permute-start.6 = (bf16[144,192]{1,0:T(8,128)(2,1)S(1)}, bf16[144,192]{1,0:T(8,128)(2,1)S(1)}, u32[]{:S(2)}, u32[]{:S(2)}) collective-permute-start(bf16[144,192]{1,0:T(8,128)(2,1)S(1)} %copy-done.30), channel_id=1, source_target_pairs={{0,2},{2,4},{4,6},{6,8},{8,10},{10,12},{12,14},{14,16},{16,18},{18... | collective-permute-start | bytes 165896 | tf_op jit(solution)/shard_map/ppermute | solution.py:374
  72.8 25.2 %collective-permute-start.7 = (bf16[144,192]{1,0:T(8,128)(2,1)S(1)}, bf16[144,192]{1,0:T(8,128)(2,1)S(1)}, u32[]{:S(2)}, u32[]{:S(2)}) collective-permute-start(bf16[144,192]{1,0:T(8,128)(2,1)S(1)} %copy-done.29), channel_id=1, source_target_pairs={{0,1},{1,0},{2,3},{3,2},{4,5},{5,4},{6,7},{7,6},{8,9},{9,8},{10,11... | collective-permute-start | bytes 165896 | tf_op jit(solution)/shard_map/ppermute | solution.py:375
  74.1 25.8 %collective-permute-start.8 = (bf16[144,192]{1,0:T(8,128)(2,1)S(1)}, bf16[144,192]{1,0:T(8,128)(2,1)S(1)}, u32[]{:S(2)}, u32[]{:S(2)}) collective-permute-start(bf16[144,192]{1,0:T(8,128)(2,1)S(1)} %copy-done.28), channel_id=1, source_target_pairs={{0,3},{1,2},{2,5},{3,4},{4,7},{5,6},{6,9},{7,8},{8,11},{9,10},{10,... | collective-permute-start | bytes 165896 | tf_op jit(solution)/shard_map/ppermute | solution.py:376
  98.0 1.8 copy-start.24
  98.0 1.8 copy-start.25
  99.8 0.6 copy-start.26
  113.4 31.4 %all-to-all-start = ((bf16[32,128,128]{2,1,0:T(8,128)(2,1)}), bf16[32,128,128]{2,1,0:T(8,128)(2,1)S(1)}, u32[]{:S(2)}, u32[]{:S(2)}) async-start(bf16[32,128,128]{2,1,0:T(8,128)(2,1)} %bitcast.182), calls=%async_computation | async-start | bytes 2097152 | tf_op jit(solution)/shard_map/all_to_all | solution.py:390
  118.8 5.5 %collective-permute-start.11 = (bf16[128,128]{1,0:T(8,128)(2,1)S(1)}, bf16[128,128]{1,0:T(8,128)(2,1)S(1)}, u32[]{:S(2)}, u32[]{:S(2)}) collective-permute-start(bf16[128,128]{1,0:T(8,128)(2,1)S(1)} %reduce_sum.25), channel_id=1, source_target_pairs={{0,1},{1,0},{2,3},{3,2},{4,5},{5,4},{6,7},{7,6},{8,9},{9,8},{10,11... | collective-permute-start | bytes 98312 | tf_op jit(solution)/shard_map/ppermute | solution.py:394
  144.8 1.9 copy-start.3
  146.7 53.1 %all-to-all-start.3 = ((bf16[32,2,128,128]{3,2,1,0:T(8,128)(2,1)}), bf16[32,2,128,128]{3,2,1,0:T(8,128)(2,1)S(1)}, u32[]{:S(2)}, u32[]{:S(2)}) async-start(bf16[32,2,128,128]{3,2,1,0:T(8,128)(2,1)} %broadcast_in_dim.10), calls=%async_computation.3 | async-start | bytes 4194304 | tf_op jit(solution)/shard_map/all_to_all | solution.py:398
  153.5 5.5 %collective-permute-start.10 = (bf16[128,128]{1,0:T(8,128)(2,1)S(1)}, bf16[128,128]{1,0:T(8,128)(2,1)S(1)}, u32[]{:S(2)}, u32[]{:S(2)}) collective-permute-start(bf16[128,128]{1,0:T(8,128)(2,1)S(1)} %reduce_sum.24), channel_id=1, source_target_pairs={{0,1},{1,0},{2,3},{3,2},{4,5},{5,4},{6,7},{7,6},{8,9},{9,8},{10,11... | collective-permute-start | bytes 98312 | tf_op jit(solution)/shard_map/ppermute | solution.py:394
  199.8 2.0 copy-start.2
  201.8 6.1 %copy-start.27 = (bf16[576,192]{1,0:T(8,128)(2,1)S(1)}, bf16[576,192]{1,0:T(8,128)(2,1)}, u32[]{:S(2)}) copy-start(bf16[576,192]{1,0:T(8,128)(2,1)} %get-tuple-element.46) | copy-start | bytes 663556
  201.8 53.5 %all-to-all-start.1 = ((bf16[32,2,128,128]{3,2,1,0:T(8,128)(2,1)}), bf16[32,2,128,128]{3,2,1,0:T(8,128)(2,1)S(1)}, u32[]{:S(2)}, u32[]{:S(2)}) async-start(bf16[32,2,128,128]{3,2,1,0:T(8,128)(2,1)} %broadcast_in_dim.9), calls=%async_computation.1 | async-start | bytes 4194304 | tf_op jit(solution)/shard_map/all_to_all | solution.py:398
  207.9 6.1 %collective-permute-start.9 = (bf16[576,192]{1,0:T(8,128)(2,1)S(1)}, bf16[576,192]{1,0:T(8,128)(2,1)S(1)}, u32[]{:S(2)}, u32[]{:S(2)}) collective-permute-start(bf16[576,192]{1,0:T(8,128)(2,1)S(1)} %copy-done.27), channel_id=1, source_target_pairs={{64,0},{128,64},{192,128},{65,1},{129,65},{193,129},{66,2},{130,66... | collective-permute-start | bytes 663560 | tf_op jit(solution)/shard_map/ppermute | solution.py:477
  227.5 1.4 copy-start.16
  260.8 1.4 copy-start.17
  265.6 1.7 copy-start.6
  265.6 1.7 copy-start.7
  269.0 2.3 copy-start.8
  269.0 2.3 copy-start.9
  269.0 2.3 copy-start.10
  269.1 2.3 copy-start.11
  271.5 1.2 copy-start.4
  272.7 1.1 copy-start.5
  272.7 2.2 copy-start.12
  272.7 2.2 copy-start.13
  272.7 3.0 %copy-start.1 = (f32[1,2,4,2,6,3312]{5,3,4,2,1,0:T(2,128)S(1)}, f32[1,2,4,2,6,3312]{5,3,4,2,1,0:T(2,128)}, u32[]{:S(2)}) copy-start(f32[1,2,4,2,6,3312]{5,3,4,2,1,0:T(2,128)} %param.19) | copy-start | bytes 3815428
